TPU v7x, 32 devices: a whole 2x2x4 slice. The times are simulated.
32 devices in a mesh: fsdp: 32 (over z, y, x, core).
Axes of the slice: x: 2, y: 2, z: 4, core: 2. Of those that a mesh axis runs over, the one named last changes fastest.
Arguments:
- block_input: bfloat16 [12288, 1152], P('fsdp'), may hold values from -6 to 6
- params: bfloat16 [1, 15241216], P(None, 'fsdp'), may hold values from -4 to 4, as said below
- cotangent: bfloat16 [12288, 1152], P('fsdp'), may hold values from -6 to 6
- segment_ids: int32 [12288], replicated, may hold values from 0 to 17, never falling along the last dimension, each value on 1 to 729 neighbouring positions
Outputs:
- activations: bfloat16 [12288, 1152], P('fsdp')
- input_grad: bfloat16 [12288, 1152], P('fsdp')
- param_grads: float32 [1, 15241216], P(None, 'fsdp')
Inputs may be any that keep to these rules, and one draw needn't show every extreme that they name: `segment_ids`: image ids never fall along the tokens; each image holds 1 to 729 tokens, one exactly 729. `params`: gains lie around one, biases and weights around zero.
All inputs are finite; a program needn't handle non-finite values.
Results may differ from a plain program's by a relative error of at most 0.012.
Values may be sent and summed in bfloat16 or wider, within the bound.
A program may use at most 320 MiB of HBM per device.

v0:
```python
import math

import jax
import jax.numpy as jnp
from jax import lax
from jax.sharding import PartitionSpec as P

D = 1152
HEADS = 16
HEAD_DIM = 72
FF = 4304
LAYERS = 1
TOK_DEV = 384
REACH = 2


EPS = 1e-06
NEG = -1e30


def passed_along(value, axis, steps):
    count = lax.axis_size(axis)
    first, last = (max(0, -steps), min(count, count - steps))
    return lax.ppermute(value, axis, [(source, source + steps) for source in range(first, last)])


def layout():
    return [
        ("ln1_gain", (D,)),
        ("ln1_bias", (D,)),
        ("w_query", (D, D)),
        ("w_key", (D, D)),
        ("w_value", (D, D)),
        ("b_query", (D,)),
        ("b_value", (D,)),
        ("w_out", (D, D)),
        ("b_out", (D,)),
        ("ln2_gain", (D,)),
        ("ln2_bias", (D,)),
        ("w_up", (D, FF)),
        ("b_up", (FF,)),
        ("w_down", (FF, D)),
        ("b_down", (D,)),
    ]


def unpack(flat_vec):
    pieces = {}
    offset = 0
    for param_name, param_shape in layout():
        length = math.prod(param_shape)
        pieces[param_name] = flat_vec[offset : offset + length].reshape(param_shape)
        offset += length
    return pieces


def pack_grads(grad_map, total_len):
    pieces = [
        grad_map[param_name].astype(jnp.float32).reshape(-1) for param_name, param_shape in layout()
    ]
    used_len = sum((math.prod(param_shape) for param_name, param_shape in layout()))
    pieces.append(jnp.zeros((total_len - used_len,), jnp.float32))
    return jnp.concatenate(pieces)


def layer_norm(values, gain_vec, bias_vec):
    centre = values - jnp.mean(values, axis=-1, keepdims=True)
    inverse = lax.rsqrt(jnp.mean(centre * centre, axis=-1, keepdims=True) + EPS)
    normed = centre * inverse
    return (normed, inverse, normed * gain_vec.astype(jnp.float32) + bias_vec.astype(jnp.float32))


def norm_back(grad_out, normed, inverse, gain_vec):
    gain_grad = jnp.sum(grad_out * normed, axis=0)
    bias_grad = jnp.sum(grad_out, axis=0)
    scaled = grad_out * gain_vec.astype(jnp.float32)
    grad_in = inverse * (
        scaled
        - jnp.mean(scaled, axis=-1, keepdims=True)
        - normed * jnp.mean(scaled * normed, axis=-1, keepdims=True)
    )
    return (grad_in, gain_grad, bias_grad)


def gelu_tanh(values):
    return jax.nn.gelu(values, approximate=True)


def mat(left, right):
    return jnp.dot(left, right, preferred_element_type=jnp.float32)


def split_heads(matrix):
    return matrix.reshape(matrix.shape[0], HEADS, HEAD_DIM).transpose(1, 0, 2)


def join_heads(stacked):
    return stacked.transpose(1, 0, 2).reshape(stacked.shape[1], HEADS * HEAD_DIM)


def neighbour_window(key_rows, value_rows):
    key_blocks = []
    value_blocks = []
    for offset in range(-REACH, REACH + 1):
        if offset == 0:
            key_near, value_near = (key_rows, value_rows)
        else:
            key_near, value_near = passed_along((key_rows, value_rows), "fsdp", -offset)
        key_blocks.append(key_near)
        value_blocks.append(value_near)
    return (jnp.concatenate(key_blocks, axis=0), jnp.concatenate(value_blocks, axis=0))


def return_key_grads(key_win_grad, value_win_grad):
    middle = REACH * TOK_DEV
    key_total = key_win_grad[middle : middle + TOK_DEV]
    value_total = value_win_grad[middle : middle + TOK_DEV]
    for offset in range(-REACH, REACH + 1):
        if offset != 0:
            first_row = (offset + REACH) * TOK_DEV
            back_key, back_value = (
                passed_along(
                    key_win_grad[first_row : first_row + TOK_DEV].astype(jnp.bfloat16),
                    "fsdp",
                    offset,
                ).astype(jnp.float32),
                passed_along(
                    value_win_grad[first_row : first_row + TOK_DEV].astype(jnp.bfloat16),
                    "fsdp",
                    offset,
                ).astype(jnp.float32),
            )
            key_total = key_total + back_key
            value_total = value_total + back_value
    return (key_total, value_total)


def attend_local(queries, key_win, value_win, allowed):
    scale = HEAD_DIM ** (-0.5)

    def one_head(inputs):
        query_one, key_one, value_one = inputs
        scores = jnp.where(allowed, mat(query_one, key_one.T) * scale, NEG)
        top_score = jnp.max(scores, axis=-1, keepdims=True)
        logsum = top_score + jnp.log(jnp.sum(jnp.exp(scores - top_score), axis=-1, keepdims=True))
        probs = jnp.exp(scores - logsum).astype(jnp.bfloat16)
        return (mat(probs, value_one).astype(jnp.bfloat16), logsum[:, 0])

    outputs, logsums = lax.map(
        one_head, (split_heads(queries), split_heads(key_win), split_heads(value_win))
    )
    return (join_heads(outputs), logsums)


def attend_local_back(queries, key_win, value_win, allowed, logsums, attended_grad):
    scale = HEAD_DIM ** (-0.5)

    def one_head(inputs):
        query_one, key_one, value_one, grad_one, log_one = inputs
        scores = jnp.where(allowed, mat(query_one, key_one.T) * scale, NEG)
        probs = jnp.exp(scores - log_one[:, None])
        probs_b = probs.astype(jnp.bfloat16)
        prob_grad = mat(grad_one, value_one.T)
        row_total = jnp.sum(probs * prob_grad, axis=-1, keepdims=True)
        score_b = (probs * (prob_grad - row_total)).astype(jnp.bfloat16)
        grad_q = mat(score_b, key_one) * scale
        grad_k = mat(score_b.T, query_one) * scale
        grad_v = mat(probs_b.T, grad_one)
        return (grad_q, grad_k, grad_v)

    grad_q, grad_k, grad_v = lax.map(
        one_head,
        (
            split_heads(queries),
            split_heads(key_win),
            split_heads(value_win),
            split_heads(attended_grad),
            logsums,
        ),
    )
    return (join_heads(grad_q), join_heads(grad_k), join_heads(grad_v))


def layer_forward(state, weights, allowed):
    normed1, inverse1, pre1 = layer_norm(state, weights["ln1_gain"], weights["ln1_bias"])
    normed_in = pre1.astype(jnp.bfloat16)
    queries = (mat(normed_in, weights["w_query"]) + weights["b_query"].astype(jnp.float32)).astype(
        jnp.bfloat16
    )
    key_rows = mat(normed_in, weights["w_key"]).astype(jnp.bfloat16)
    value_rows = (
        mat(normed_in, weights["w_value"]) + weights["b_value"].astype(jnp.float32)
    ).astype(jnp.bfloat16)
    key_win, value_win = neighbour_window(key_rows, value_rows)
    attended, logsums = attend_local(queries, key_win, value_win, allowed)
    mid = state + (mat(attended, weights["w_out"]) + weights["b_out"].astype(jnp.float32))
    normed2, inverse2, pre2 = layer_norm(mid, weights["ln2_gain"], weights["ln2_bias"])
    normed_mid = pre2.astype(jnp.bfloat16)
    pre_act = mat(normed_mid, weights["w_up"]) + weights["b_up"].astype(jnp.float32)
    hidden = gelu_tanh(pre_act).astype(jnp.bfloat16)
    out_state = mid + (mat(hidden, weights["w_down"]) + weights["b_down"].astype(jnp.float32))
    saved = (
        normed1,
        inverse1,
        normed_in,
        queries,
        key_win,
        value_win,
        attended,
        logsums,
        normed2,
        inverse2,
        normed_mid,
        pre_act,
        hidden,
    )
    return (out_state, saved)


def layer_backward(grad_out, weights, saved, allowed):
    (
        normed1,
        inverse1,
        normed_in,
        queries,
        key_win,
        value_win,
        attended,
        logsums,
        normed2,
        inverse2,
        normed_mid,
        pre_act,
        hidden,
    ) = saved
    grads = {}
    grad_b = grad_out.astype(jnp.bfloat16)
    grads["w_down"] = mat(hidden.T, grad_b)
    grads["b_down"] = jnp.sum(grad_out, axis=0)
    hidden_grad = mat(grad_b, weights["w_down"].T)
    pre_grad = jax.vjp(gelu_tanh, pre_act)[1](hidden_grad)[0]
    pre_b = pre_grad.astype(jnp.bfloat16)
    grads["w_up"] = mat(normed_mid.T, pre_b)
    grads["b_up"] = jnp.sum(pre_grad, axis=0)
    norm_grad = mat(pre_b, weights["w_up"].T)
    mid_part, grads["ln2_gain"], grads["ln2_bias"] = norm_back(
        norm_grad, normed2, inverse2, weights["ln2_gain"]
    )
    mid_grad = grad_out + mid_part
    mid_b = mid_grad.astype(jnp.bfloat16)
    grads["w_out"] = mat(attended.T, mid_b)
    grads["b_out"] = jnp.sum(mid_grad, axis=0)
    attended_grad = mat(mid_b, weights["w_out"].T).astype(jnp.bfloat16)
    grad_q, key_win_grad, value_win_grad = attend_local_back(
        queries, key_win, value_win, allowed, logsums, attended_grad
    )
    grad_k, grad_v = return_key_grads(key_win_grad, value_win_grad)
    query_b = grad_q.astype(jnp.bfloat16)
    key_b = grad_k.astype(jnp.bfloat16)
    value_b = grad_v.astype(jnp.bfloat16)
    grads["w_query"] = mat(normed_in.T, query_b)
    grads["w_key"] = mat(normed_in.T, key_b)
    grads["w_value"] = mat(normed_in.T, value_b)
    grads["b_query"] = jnp.sum(grad_q, axis=0)
    grads["b_value"] = jnp.sum(grad_v, axis=0)
    in_grad = (
        mat(query_b, weights["w_query"].T)
        + mat(key_b, weights["w_key"].T)
        + mat(value_b, weights["w_value"].T)
    )
    in_part, grads["ln1_gain"], grads["ln1_bias"] = norm_back(
        in_grad, normed1, inverse1, weights["ln1_gain"]
    )
    return (mid_grad + in_part, grads)


def shards(block_input, params, cotangent, segment_ids):
    device_count = lax.axis_size("fsdp")
    my_index = lax.axis_index("fsdp")
    margin = REACH * TOK_DEV
    window = (2 * REACH + 1) * TOK_DEV
    seg_pad = jnp.pad(segment_ids, (margin, margin), constant_values=-1)
    seg_query = lax.dynamic_slice_in_dim(segment_ids, my_index * TOK_DEV, TOK_DEV, 0)
    seg_keys = lax.dynamic_slice_in_dim(seg_pad, my_index * TOK_DEV, window, 0)
    allowed = seg_query[:, None] == seg_keys[None, :]
    total_len = params.shape[1] * device_count
    state = block_input.astype(jnp.float32)
    gathered = []
    layer_idx = 0
    flat_params = lax.all_gather(params[layer_idx], "fsdp", axis=0, tiled=True)
    gathered.append(flat_params)
    state, saved = layer_forward(state, unpack(flat_params), allowed)
    saved_list = [saved]
    activations = state.astype(jnp.bfloat16)
    grad = cotangent.astype(jnp.float32)
    flat_grads = [None] * LAYERS
    for layer_idx in reversed(range(LAYERS)):
        flat_params = lax.all_gather(params[layer_idx], "fsdp", axis=0, tiled=True)
        grad, grad_map = layer_backward(grad, unpack(flat_params), saved_list[layer_idx], allowed)
        packed = pack_grads(grad_map, total_len).reshape(device_count, total_len // device_count)
        received = lax.all_to_all(
            packed.astype(jnp.bfloat16), "fsdp", split_axis=0, concat_axis=0, tiled=True
        ).astype(packed.dtype)
        flat_grads[layer_idx] = jnp.sum(received, axis=0)
    param_grads = jnp.stack(flat_grads)
    return (activations, grad.astype(jnp.bfloat16), param_grads)


def solution(mesh):
    return jax.shard_map(
        shards,
        mesh=mesh,
        in_specs=(P("fsdp", None), P(None, "fsdp"), P("fsdp", None), P()),
        out_specs=(P("fsdp", None), P("fsdp", None), P(None, "fsdp")),
        check_vma=False,
    )
```

profile of v0, /device:TPU:0, one launch (start us, length us, event | category | flops | bytes accessed | tf_op | source)
XLA Modules:
  0.0 2954.0 jit_solution(8297394182015915565)
XLA Ops:
  11.9 328.0 %all-gather.3.cloned.1.call-done = bf16[1,15241216]{1,0:T(2,128)(2,1)} async-done(((bf16[1,476288]{1,0:T(2,128)(2,1)}), bf16[1,15241216]{1,0:T(2,128)(2,1)}) %all-gather.3.cloned.1.call-update) | async-done | bytes 30482448 | tf_op jit(solution)/shard_map/all_gather | solution.py:290
  339.9 86.3 %slice_reduce_fusion.2 = (bf16[1327104]{0:T(1024)(128)(2,1)}, bf16[1327104]{0:T(1024)(128)(2,1)}, bf16[1327104]{0:T(1024)(128)(2,1)}, bf16[1327104]{0:T(1024)(128)(2,1)S(1)}) fusion(bf16[1,15241216]{1,0:T(2,128)(2,1)} %all-gather.3.cloned.1.call-done), kind=kLoop, calls=%fused_computation.76 | loop fusion | bytes 21233664 | tf_op jit(solution)/shard_map/slice | solution.py:52
  446.9 6.6 reshape.194
  464.9 218.0 %slice_reduce_fusion.1 = (bf16[4958208]{0:T(1024)(128)(2,1)}, bf16[4958208]{0:T(1024)(128)(2,1)}) fusion(bf16[1,15241216]{1,0:T(2,128)(2,1)} %all-gather.3.cloned.1.call-done), kind=kLoop, calls=%fused_computation.59 | loop fusion | bytes 39665664 | tf_op jit(solution)/shard_map/slice | solution.py:52
  683.0 19.2 reshape.201
  702.2 10.5 fusion.112
  719.1 20.1 reshape.200
  762.6 19.6 collective-permute-done.3
  783.2 6.7 copy.24
  789.9 8.4 copy.27
  812.3 8.3 copy.28
  820.6 95.6 %while.28 = (s32[]{:T(128)}, bf16[16,384,72]{1,2,0:T(8,128)(2,1)}, f32[16,384]{1,0:T(8,128)}, bf16[16,384,72]{2,1,0:T(8,128)(2,1)S(1)}, bf16[16,1920,72]{2,1,0:T...) while((s32[]{:T(128)}, bf16[16,384,72]{1,2,0:T(8,128)(2,1)}, ...), condition=%wide.region_5.6_spmd.clone, body=%wide.region_2.5_spmd.clone.sunk | while | flops 218262144 | bytes 10013297 | solution.py:149
  921.5 18.8 fusion.103
  940.4 8.7 multiply_reduce_fusion.1
  957.1 8.7 convolution_convert_fusion
  967.1 170.4 %while.29 = (s32[]{:T(128)}, f32[16,384,72]{1,2,0:T(8,128)S(1)}, f32[16,1920,72]{1,2,0:T(8,128)}, f32[16,1920,72]{1,2,0:T(8,128)}, bf16[16,384,72]{2,1,0:T(8,128...) while((s32[]{:T(128)}, f32[16,384,72]{1,2,0:T(8,128)S(1)}, ...), condition=%wide.region_12.13_spmd.clone, body=%wide.region_10.12_spmd.clone.sunk | while | flops 538379904 | bytes 25138816 | solution.py:171
  1137.5 11.5 convolution_convert_fusion.1
  1164.8 8.5 collective-permute-start.11
  1179.6 48.7 %collective-permute-done.15 = bf16[384,1152]{0,1:T(8,128)(2,1)S(1)} collective-permute-done((bf16[384,1152]{0,1:T(8,128)(2,1)S(1)}, bf16[384,1152]{0,1:T(8,128)(2,1)S(1)}, u32[]{:S(2)}, u32[]{:S(2)}) %collective-permute-start.15) | collective-permute-done | bytes 884768 | tf_op jit(solution)/shard_map/ppermute | solution.py:24
  1251.9 18.7 reshape.208
  1270.6 14.1 copy.34
  1284.7 22.6 reshape.207
  1340.0 446.7 %concatenate.12 = bf16[15241216]{0:T(1024)(128)(2,1)} concatenate(bf16[1152]{0:T(1024)(128)(2,1)} %get-tuple-element.200, bf16[1152]{0:T(1024)(128)(2,1)} %get-tuple-element.205, bf16[1327104]{0:T(1024)(128)(2,1)S(1)} %reshape.203, bf16[1327104]{0:T(1024)(128)(2,1)} %reshape.204, bf16[1327104]{0:T(1024)(128)(2,1)} %reshape.205, bf16[1152]{0:T(1024)(128)(2,1)} %reduce_sum.193, ...), dimensions={0} | concatenate | bytes 60964864 | tf_op jit(solution)/shard_map/concatenate | solution.py:63
  1786.7 56.4 %convert_element_type.222 = bf16[32,1,476288]{2,1,0:T(2,128)(2,1)} reshape(bf16[15241216]{0:T(1024)(128)(2,1)} %concatenate.12) | data formatting | bytes 60964864 | tf_op jit(solution)/shard_map/convert_element_type | solution.py:302
  1843.6 179.9 %reduce.35 = bf16[32,476288]{1,0:T(8,128)(2,1)} reduce(bf16[32,1,476288]{2,1,0:T(2,128)(2,1)} %convert_element_type.222, bf16[]{:T(256)} %broadcast.170), dimensions={1}, to_apply=%convert_element_type.222.reduce_sub_computation | reduce | bytes 60964864 | tf_op jit(solution)/shard_map/convert_element_type | solution.py:302
  2023.5 53.4 %reshape.256 = bf16[32,2,238144]{2,1,0:T(2,128)(2,1)} reshape(bf16[32,476288]{1,0:T(8,128)(2,1)} %reduce.35) | data formatting | bytes 60964864
  2077.0 13.8 all-to-all-start
  2090.8 11.4 fusion.58
  2103.9 665.7 %all-to-all-done = bf16[32,2,238144]{2,1,0:T(2,128)(2,1)} async-done(((bf16[32,2,238144]{2,1,0:T(2,128)(2,1)}), bf16[32,2,238144]{2,1,0:T(2,128)(2,1)}, u32[]{:S(2)}, u32[]{:S(2)}) %all-to-all-start) | async-done | bytes 30482464 | tf_op jit(solution)/shard_map/all_to_all | solution.py:301
  2769.5 99.1 %reshape.257 = bf16[32,1,476288]{2,1,0:T(2,128)(2,1)} reshape(bf16[32,2,238144]{2,1,0:T(2,128)(2,1)} %all-to-all-done) | data formatting | bytes 60964864
  2868.6 68.6 %convert_reduce_fusion = f32[476288]{0:T(1024)S(1)} fusion(bf16[32,1,476288]{2,1,0:T(2,128)(2,1)} %reshape.257), kind=kLoop, calls=%fused_computation.57 | loop fusion | flops 30006144 | bytes 32387584 | tf_op jit(solution)/shard_map/reduce_sum | solution.py:304
  2937.3 9.7 stack.3
  (410 shorter events, 441.8 us)
Async XLA Ops:
  7.2 332.7 %all-gather.3.cloned.1.call-start = ((), (), s32[]{:S(2)}) async-start(), calls=%async_computation.1 | async-start | bytes 62870016 | tf_op jit(solution)/shard_map/all_gather | solution.py:290
  11.0 1318.8 %copy-start.26 = (f32[384]{0:T(512)}, f32[384]{0:T(512)S(1)}, u32[]{:S(2)}) copy-start(f32[384]{0:T(512)S(1)} %broadcast_multiply_fusion.5) | copy-start | bytes 4612
  438.2 365.4 %collective-permute-start.7 = (bf16[384,1152]{1,0:T(8,128)(2,1)}, bf16[384,1152]{1,0:T(8,128)(2,1)}, u32[]{:S(2)}, u32[]{:S(2)}) collective-permute-start(bf16[384,1152]{1,0:T(8,128)(2,1)} %fusion.57), channel_id=1, source_target_pairs={{2,0},{3,1},{4,2},{5,3},{6,4},{7,5},{8,6},{9,7},{10,8},{11,9},{12,... | collective-permute-start | bytes 2654216 | tf_op jit(solution)/shard_map/ppermute | solution.py:24
  439.5 358.8 %collective-permute-start.5 = (bf16[384,1152]{1,0:T(8,128)(2,1)}, bf16[384,1152]{1,0:T(8,128)(2,1)}, u32[]{:S(2)}, u32[]{:S(2)}) collective-permute-start(bf16[384,1152]{1,0:T(8,128)(2,1)} %fusion.57), channel_id=1, source_target_pairs={{0,1},{1,2},{2,3},{3,4},{4,5},{5,6},{6,7},{7,8},{8,9},{9,10},{10,1... | collective-permute-start | bytes 2654216 | tf_op jit(solution)/shard_map/ppermute | solution.py:24
  442.6 315.6 %collective-permute-start.4 = (bf16[384,1152]{1,0:T(8,128)(2,1)}, bf16[384,1152]{1,0:T(8,128)(2,1)}, u32[]{:S(2)}, u32[]{:S(2)}) collective-permute-start(bf16[384,1152]{1,0:T(8,128)(2,1)} %fusion.57), channel_id=1, source_target_pairs={{0,2},{1,3},{2,4},{3,5},{4,6},{5,7},{6,8},{7,9},{8,10},{9,11},{10,... | collective-permute-start | bytes 2654216 | tf_op jit(solution)/shard_map/ppermute | solution.py:24
  457.7 294.8 %collective-permute-start.1 = (bf16[384,1152]{1,0:T(8,128)(2,1)}, bf16[384,1152]{1,0:T(8,128)(2,1)}, u32[]{:S(2)}, u32[]{:S(2)}) collective-permute-start(bf16[384,1152]{1,0:T(8,128)(2,1)} %convolution_convert_fusion.7), channel_id=1, source_target_pairs={{0,1},{1,2},{2,3},{3,4},{4,5},{5,6},{6,7},{7,8},{8,9},{9,10},{10,1... | collective-permute-start | bytes 2654216 | tf_op jit(solution)/shard_map/ppermute | solution.py:24
  462.7 286.3 %collective-permute-start = (bf16[384,1152]{1,0:T(8,128)(2,1)}, bf16[384,1152]{1,0:T(8,128)(2,1)}, u32[]{:S(2)}, u32[]{:S(2)}) collective-permute-start(bf16[384,1152]{1,0:T(8,128)(2,1)} %convolution_convert_fusion.7), channel_id=1, source_target_pairs={{0,2},{1,3},{2,4},{3,5},{4,6},{5,7},{6,8},{7,9},{8,10},{9,11},{10,... | collective-permute-start | bytes 2654216 | tf_op jit(solution)/shard_map/ppermute | solution.py:24
  749.1 12.5 collective-permute-start.2
  752.5 29.6 %collective-permute-start.3 = (bf16[384,1152]{1,0:T(8,128)(2,1)}, bf16[384,1152]{1,0:T(8,128)(2,1)S(1)}, u32[]{:S(2)}, u32[]{:S(2)}) collective-permute-start(bf16[384,1152]{1,0:T(8,128)(2,1)} %convolution_convert_fusion.7), channel_id=1, source_target_pairs={{2,0},{3,1},{4,2},{5,3},{6,4},{7,5},{8,6},{9,7},{10,8},{11,9},{12,... | collective-permute-start | bytes 2654216 | tf_op jit(solution)/shard_map/ppermute | solution.py:24
  758.1 44.4 %collective-permute-start.6 = (bf16[384,1152]{1,0:T(8,128)(2,1)}, bf16[384,1152]{1,0:T(8,128)(2,1)S(1)}, u32[]{:S(2)}, u32[]{:S(2)}) collective-permute-start(bf16[384,1152]{1,0:T(8,128)(2,1)} %fusion.57), channel_id=1, source_target_pairs={{1,0},{2,1},{3,2},{4,3},{5,4},{6,5},{7,6},{8,7},{9,8},{10,9},{11,1... | collective-permute-start | bytes 2654216 | tf_op jit(solution)/shard_map/ppermute | solution.py:24
  820.6 96.8 %copy-start.42 = (f32[1152]{0:T(1024)S(1)}, f32[1152]{0:T(1024)}, u32[]{:S(2)}) copy-start(f32[1152]{0:T(1024)} %get-tuple-element.186) | copy-start | bytes 13828
  917.4 23.0 slice-start
  921.1 27.9 copy-start.3
  921.2 27.9 copy-start.28
  921.5 27.6 copy-start.33
  921.5 18.9 slice-start.1
  921.5 18.9 slice-start.2
  967.1 170.4 %copy-start.10 = (bf16[384,1152]{1,0:T(8,128)(2,1)S(1)}, bf16[384,1152]{1,0:T(8,128)(2,1)}, u32[]{:S(2)}) copy-start(bf16[384,1152]{1,0:T(8,128)(2,1)} %param.10) | copy-start | bytes 2654212
  1137.5 11.5 copy-start
  1150.7 77.6 %collective-permute-start.15 = (bf16[384,1152]{0,1:T(8,128)(2,1)S(1)}, bf16[384,1152]{0,1:T(8,128)(2,1)S(1)}, u32[]{:S(2)}, u32[]{:S(2)}) collective-permute-start(bf16[384,1152]{0,1:T(8,128)(2,1)S(1)} %bitcast.171), channel_id=1, source_target_pairs={{0,2},{1,3},{2,4},{3,5},{4,6},{5,7},{6,8},{7,9},{8,10},{9,11},{10,... | collective-permute-start | bytes 2654216 | tf_op jit(solution)/shard_map/ppermute | solution.py:24
  1155.0 74.6 %collective-permute-start.12 = (bf16[384,1152]{0,1:T(8,128)(2,1)S(1)}, bf16[384,1152]{0,1:T(8,128)(2,1)S(1)}, u32[]{:S(2)}, u32[]{:S(2)}) collective-permute-start(bf16[384,1152]{0,1:T(8,128)(2,1)S(1)} %bitcast.170), channel_id=1, source_target_pairs={{2,0},{3,1},{4,2},{5,3},{6,4},{7,5},{8,6},{9,7},{10,8},{11,9},{12,... | collective-permute-start | bytes 2654216 | tf_op jit(solution)/shard_map/ppermute | solution.py:24
  1156.3 75.5 %collective-permute-start.14 = (bf16[384,1152]{0,1:T(8,128)(2,1)S(1)}, bf16[384,1152]{0,1:T(8,128)(2,1)S(1)}, u32[]{:S(2)}, u32[]{:S(2)}) collective-permute-start(bf16[384,1152]{0,1:T(8,128)(2,1)S(1)} %bitcast.169), channel_id=1, source_target_pairs={{0,1},{1,2},{2,3},{3,4},{4,5},{5,6},{6,7},{7,8},{8,9},{9,10},{10,1... | collective-permute-start | bytes 2654216 | tf_op jit(solution)/shard_map/ppermute | solution.py:24
  1157.7 149.7 %collective-permute-start.13 = (bf16[384,1152]{0,1:T(8,128)(2,1)}, bf16[384,1152]{0,1:T(8,128)(2,1)}, u32[]{:S(2)}, u32[]{:S(2)}) collective-permute-start(bf16[384,1152]{0,1:T(8,128)(2,1)} %bitcast.24), channel_id=1, source_target_pairs={{1,0},{2,1},{3,2},{4,3},{5,4},{6,5},{7,6},{8,7},{9,8},{10,9},{11,1... | collective-permute-start | bytes 2654216 | tf_op jit(solution)/shard_map/ppermute | solution.py:24
  1164.8 157.0 %collective-permute-start.11 = (bf16[384,1152]{0,1:T(8,128)(2,1)}, bf16[384,1152]{0,1:T(8,128)(2,1)}, u32[]{:S(2)}, u32[]{:S(2)}) collective-permute-start(bf16[384,1152]{0,1:T(8,128)(2,1)} %bitcast.20), channel_id=1, source_target_pairs={{0,2},{1,3},{2,4},{3,5},{4,6},{5,7},{6,8},{7,9},{8,10},{9,11},{10,... | collective-permute-start | bytes 2654216 | tf_op jit(solution)/shard_map/ppermute | solution.py:24
  1228.3 93.6 %collective-permute-start.8 = (bf16[384,1152]{0,1:T(8,128)(2,1)}, bf16[384,1152]{0,1:T(8,128)(2,1)}, u32[]{:S(2)}, u32[]{:S(2)}) collective-permute-start(bf16[384,1152]{0,1:T(8,128)(2,1)} %bitcast.17), channel_id=1, source_target_pairs={{2,0},{3,1},{4,2},{5,3},{6,4},{7,5},{8,6},{9,7},{10,8},{11,9},{12,... | collective-permute-start | bytes 2654216 | tf_op jit(solution)/shard_map/ppermute | solution.py:24
  1229.6 92.3 %collective-permute-start.10 = (bf16[384,1152]{0,1:T(8,128)(2,1)}, bf16[384,1152]{0,1:T(8,128)(2,1)}, u32[]{:S(2)}, u32[]{:S(2)}) collective-permute-start(bf16[384,1152]{0,1:T(8,128)(2,1)} %bitcast.19), channel_id=1, source_target_pairs={{0,1},{1,2},{2,3},{3,4},{4,5},{5,6},{6,7},{7,8},{8,9},{9,10},{10,1... | collective-permute-start | bytes 2654216 | tf_op jit(solution)/shard_map/ppermute | solution.py:24
  1232.7 89.2 %collective-permute-start.9 = (bf16[384,1152]{0,1:T(8,128)(2,1)}, bf16[384,1152]{0,1:T(8,128)(2,1)}, u32[]{:S(2)}, u32[]{:S(2)}) collective-permute-start(bf16[384,1152]{0,1:T(8,128)(2,1)} %bitcast.18), channel_id=1, source_target_pairs={{1,0},{2,1},{3,2},{4,3},{5,4},{6,5},{7,6},{8,7},{9,8},{10,9},{11,1... | collective-permute-start | bytes 2654216 | tf_op jit(solution)/shard_map/ppermute | solution.py:24
  2076.9 13.8 copy-start.5
  2076.9 13.8 copy-start.35
  2077.0 692.6 %all-to-all-start = ((bf16[32,2,238144]{2,1,0:T(2,128)(2,1)}), bf16[32,2,238144]{2,1,0:T(2,128)(2,1)}, u32[]{:S(2)}, u32[]{:S(2)}) async-start(bf16[32,2,238144]{2,1,0:T(2,128)(2,1)} %reshape.256), calls=%async_computation | async-start | bytes 60981248 | tf_op jit(solution)/shard_map/all_to_all | solution.py:301
  2090.8 11.5 copy-start.7
  2090.8 11.5 copy-start.15
  (37 other events, 174.7 us)
Sparse Core Ops, SparseCore 0:
  10.9 328.9 all-gather.2
where the time goes:
time: 3010 us; the launch traced here: 2950 us
  local copies, waits for them, and re-layouts  1210 us (40%)
  waiting for transfers between devices  1060 us (35%)
  matrix products  326 us (11%)
  other arithmetic  284 us (9%)
  starting transfers between devices  55.3 us (2%)
    all_to_all x1, waiting for transfers between devices, shards(): lax.all_to_all(packed.astype(jnp.bfloat16), 'fsdp', split_axis=0, concat_...  666 us
    concatenate x1, local copies, waits for them, and re-layouts, pack_grads(): return jnp.concatenate(pieces)  447 us
    all_gather x1, waiting for transfers between devices, shards(): flat_params = lax.all_gather(params[layer_idx], 'fsdp', axis=0, tiled=True)  328 us
    dot_general x130, matrix products, mat(): return jnp.dot(left, right, preferred_element_type=jnp.float32)  326 us
    slice x2, local copies, waits for them, and re-layouts, unpack(): pieces[param_name] = flat_vec[offset:offset + length].reshape(param_shape)  304 us
    unnamed x115, local copies, waits for them, and re-layouts  189 us
    convert_element_type x1, other arithmetic, shards(): packed.astype(jnp.bfloat16)  180 us
    reduce_sum x1, other arithmetic, shards(): flat_grads[layer_idx] = jnp.sum(received, axis=0)  68.6 us
  transfers between devices with their start and end apart: 18, of which 4 were waited for; matrix products, arithmetic and copies ran while one was open for 15% of the time, Pallas kernels for 0%

commit v1 on v0

v1 whole, which is shorter than its diff:
```python
import functools
import math

import jax
import jax.numpy as jnp
import numpy as np
from jax import lax
from jax.experimental import pallas as pl
from jax.experimental.pallas import tpu as pltpu
from jax.sharding import PartitionSpec as P

D = 1152
HEADS = 16
HEAD_DIM = 72
FF = 4304
REACH = 2


EPS = 1e-06
NEG = -1e30
LANES = 128
ROWS = 16
DC = D // LANES
FC = -(-FF // LANES)
WIDE = FF * ROWS // LANES
HEAD = 544
KIND_A, KIND_D, KIND_L2, KIND_L3, KIND_B = 1, 2, 3, 4, 5
MESH = pl.DeviceIdType.MESH


def units():
    found = []
    offset = 0

    def matrix(name, kind, rows, width, tiles):
        nonlocal offset
        for row in range(0, rows, ROWS):
            found.append((name, kind, offset + row * width, tiles))
        offset += rows * width

    def vectors(name, kind, length, tiles):
        nonlocal offset
        found.append((name, kind, offset, tiles))
        offset += length

    vectors("vec1", KIND_L2, 2 * D, 2)
    matrix("w_query", KIND_A, D, D, DC)
    matrix("w_key", KIND_A, D, D, DC)
    matrix("w_value", KIND_A, D, D, DC)
    vectors("vec2", KIND_L2, 2 * D, 2)
    matrix("w_out", KIND_A, D, D, DC)
    vectors("vec3", KIND_L2, 3 * D, 2)
    matrix("w_up", KIND_B, D, FF, FC)
    vectors("vec4", KIND_L3, FF, 3)
    matrix("w_down", KIND_D, FF, D, DC)
    vectors("vec5", KIND_D, D, DC)
    return found


def unit_width(name):
    return {"vec1": 2 * D, "vec2": 2 * D, "vec3": 3 * D, "vec4": FF, "vec5": D, "w_up": ROWS * FF}.get(
        name, ROWS * D
    )


def wire_plan(count, shard):
    blocks = [[] for _ in range(count)]
    where = {}
    used = [0] * count
    tails = [0] * count
    for name, kind, first, tiles in units():
        owner = first // shard
        where.setdefault(name, []).append((owner, used[owner], tiles))
        blocks[owner].append((kind, (first - owner * shard) // LANES, used[owner]))
        used[owner] += tiles
        tails[owner] = max(0, first + unit_width(name) - (owner + 1) * shard)
    block = max(used)
    block += block % 2
    most = max(len(b) for b in blocks)
    table = np.zeros((count, 3 * most), np.int32)
    for owner, entries in enumerate(blocks):
        for i, entry in enumerate(entries):
            table[owner, 3 * i : 3 * i + 3] = entry
    return where, block, table, np.array(tails, np.int32)


def lane_iota(rows):
    return lax.broadcasted_iota(jnp.int32, (rows, LANES), 1)


def wide_rows():
    return [divmod(row * FF, LANES) for row in range(ROWS)]


SKEW = (D * 0 + 80) % LANES


def rows_from_line(line_ref, flat_ref, first, rows):
    step = 8 * LANES

    @pl.loop(0, rows // 8)
    def _(i):
        part = line_ref[:, pl.ds(pl.multiple_of(i * step, step), step)].astype(jnp.float32)
        flat_ref[pl.ds(first + i * 8, 8)] = part.reshape(8, LANES)

    for row in range(rows // 8 * 8, rows):
        flat_ref[pl.ds(first + row, 1)] = line_ref[:, row * LANES : (row + 1) * LANES].astype(jnp.float32)


def line_from_rows(flat_ref, line_ref, first, rows):
    step = 8 * LANES

    @pl.loop(0, rows // 8)
    def _(i):
        part = flat_ref[pl.ds(first + i * 8, 8)]
        line_ref[:, pl.ds(pl.multiple_of(i * step, step), step)] = part.reshape(1, step)

    for row in range(rows // 8 * 8, rows):
        line_ref[:, row * LANES : (row + 1) * LANES] = flat_ref[pl.ds(first + row, 1)]


def to_tiles_kernel(entries, table_ref, line_ref, head_ref, tile_ref, stage_ref, flat_ref):
    rows = line_ref.shape[1] // LANES
    rows_from_line(line_ref, flat_ref, 0, rows)
    rows_from_line(head_ref, flat_ref, rows, HEAD)

    def unit(i, _):
        kind, src, dst = (table_ref[3 * i + j] for j in range(3))

        @pl.when(kind == KIND_A)
        def _():
            for c in range(DC):
                tile_ref[dst + c] = flat_ref[pl.ds(src + c, ROWS, stride=DC), :].astype(jnp.bfloat16)

        @pl.when(kind == KIND_D)
        def _():
            lane = lane_iota(ROWS)
            for c in range(DC):
                here = flat_ref[pl.ds(src + c, ROWS, stride=DC), :]
                after = flat_ref[pl.ds(src + c + 1, ROWS, stride=DC), :]
                both = jnp.where(lane >= SKEW, here, after)
                tile_ref[dst + c] = pltpu.roll(both, LANES - SKEW, 1).astype(jnp.bfloat16)

        for code, tiles in ((KIND_L2, 2), (KIND_L3, 3)):

            @pl.when(kind == code)
            def _():
                for j in range(tiles):
                    tile_ref[dst + j] = flat_ref[pl.ds(src + ROWS * j, ROWS), :].astype(jnp.bfloat16)

        @pl.when(kind == KIND_B)
        def _():
            tall = 8 * pl.cdiv(FC, 8)
            lane = lane_iota(tall)
            row = lax.broadcasted_iota(jnp.int32, (tall, LANES), 0)
            keep = (row < FC - 1) | (lane < FF % LANES)
            for r, (base, skew) in enumerate(wide_rows()):
                part = flat_ref[pl.ds(src + base, tall), :]
                if skew:
                    after = flat_ref[pl.ds(src + base + 1, tall), :]
                    part = pltpu.roll(jnp.where(lane >= skew, part, after), LANES - skew, 1)
                stage_ref[pl.ds(r, tall, stride=ROWS), :] = jnp.where(keep, part, 0.0)
            for c in range(FC):
                tile_ref[dst + c] = stage_ref[pl.ds(ROWS * c, ROWS), :].astype(jnp.bfloat16)

        return 0

    lax.fori_loop(0, entries, unit, 0)


def to_flat_kernel(entries, table_ref, tile_ref, line_ref, tail_ref, stage_ref, flat_ref):
    flat_ref[...] = jnp.zeros_like(flat_ref)

    def unit(i, _):
        kind, src, dst = (table_ref[3 * i + j] for j in range(3))

        @pl.when(kind == KIND_A)
        def _():
            for c in range(DC):
                flat_ref[pl.ds(src + c, ROWS, stride=DC), :] = tile_ref[dst + c]

        @pl.when(kind == KIND_D)
        def _():
            lane = lane_iota(ROWS)
            for c in range(DC):
                turned = pltpu.roll(tile_ref[dst + c], SKEW, 1)
                for step, keep in ((0, lane >= SKEW), (1, lane < SKEW)):
                    at = pl.ds(src + c + step, ROWS, stride=DC)
                    flat_ref[at, :] = jnp.where(keep, turned, flat_ref[at, :])

        for code, tiles in ((KIND_L2, 2), (KIND_L3, 3)):

            @pl.when(kind == code)
            def _():
                for j in range(tiles):
                    flat_ref[pl.ds(src + ROWS * j, ROWS), :] = tile_ref[dst + j]

        @pl.when(kind == KIND_B)
        def _():
            tall = 8 * pl.cdiv(FC, 8)
            lane = lane_iota(tall)
            row = lax.broadcasted_iota(jnp.int32, (tall, LANES), 0)
            for c in range(FC):
                stage_ref[pl.ds(ROWS * c, ROWS), :] = tile_ref[dst + c]
            for r, (base, skew) in enumerate(wide_rows()):
                turned = stage_ref[pl.ds(r, tall, stride=ROWS), :]
                if skew:
                    turned = pltpu.roll(turned, skew, 1)
                for step in range(2 if skew else 1):
                    entry = row * LANES + lane + (step * LANES - skew)
                    keep = (lane < skew if step else lane >= skew) & (entry < FF)
                    at = pl.ds(src + base + step, tall)
                    flat_ref[at, :] = jnp.where(keep, turned, flat_ref[at, :])

        return 0

    lax.fori_loop(0, entries, unit, 0)
    rows = line_ref.shape[1] // LANES
    line_from_rows(flat_ref, line_ref, 0, rows)
    line_from_rows(flat_ref, tail_ref, rows, HEAD)


def my_row(table):
    return lax.dynamic_index_in_dim(jnp.asarray(table), lax.axis_index("fsdp"), 0, keepdims=False)


def relayout_scratch(rows):
    return [
        pltpu.VMEM((ROWS * 8 * pl.cdiv(FC, 8), LANES), jnp.float32),
        pltpu.VMEM((8 * pl.cdiv(rows + HEAD + 8, 8), LANES), jnp.float32),
    ]


def to_tiles(line, plan):
    where, block, table, tails = plan
    count = lax.axis_size("fsdp")
    head = lax.ppermute(line[:, : HEAD * LANES], "fsdp", [(i, (i - 1) % count) for i in range(count)])
    vmem = pl.BlockSpec(memory_space=pltpu.VMEM)
    return pl.pallas_call(
        functools.partial(to_tiles_kernel, table.shape[1] // 3),
        out_shape=jax.ShapeDtypeStruct((block, ROWS, LANES), jnp.bfloat16),
        grid_spec=pltpu.PrefetchScalarGridSpec(
            num_scalar_prefetch=1, grid=(1,), in_specs=[vmem, vmem], out_specs=vmem,
            scratch_shapes=relayout_scratch(line.shape[1] // LANES),
        ),
        name="to_tiles",
    )(my_row(table), line, head)


def to_flat(tiles, plan, length):
    where, block, table, tails = plan
    count = lax.axis_size("fsdp")
    vmem = pl.BlockSpec(memory_space=pltpu.VMEM)
    line, tail = pl.pallas_call(
        functools.partial(to_flat_kernel, table.shape[1] // 3),
        out_shape=(jax.ShapeDtypeStruct((1, length), jnp.float32), jax.ShapeDtypeStruct((1, HEAD * LANES), jnp.float32)),
        grid_spec=pltpu.PrefetchScalarGridSpec(
            num_scalar_prefetch=1, grid=(1,), in_specs=[vmem], out_specs=[vmem, vmem],
            scratch_shapes=relayout_scratch(length // LANES),
        ),
        name="to_flat",
    )(my_row(table), tiles)
    tail = lax.ppermute(tail, "fsdp", [(i, (i + 1) % count) for i in range(count)])
    entry = lax.broadcasted_iota(jnp.int32, tail.shape, 1)
    first = jnp.where(entry < my_row(np.roll(tails, 1)), tail, line[:, : HEAD * LANES])
    return lax.dynamic_update_slice(line, first, (0, 0))


def place(me):
    return lax.rem(me, 2), lax.rem(me // 2, 2), lax.rem(me // 4, 2), me // 8


def index_of(core, x, y, z):
    return ((z * 2 + y) * 2 + x) * 2 + core


def greet(devices_and_conditions):
    barrier = pltpu.get_barrier_semaphore()
    for device, present in devices_and_conditions:
        if present is None:
            pl.semaphore_signal(barrier, inc=1, device_id=(device,), device_id_type=MESH)
        else:

            @pl.when(present)
            def _():
                pl.semaphore_signal(barrier, inc=1, device_id=(device,), device_id_type=MESH)

    present = [1 if p is None else p.astype(jnp.int32) for _, p in devices_and_conditions]
    pl.semaphore_wait(barrier, sum(present))


def scatter_kernel(
    depth, part_ref, out_ref, held, mates, halfs, fulls, lines, load_sem, mate_send, mate_recv, half_send, half_recv, full_send, full_recv, line_send, line_recv
):
    me = lax.axis_index("fsdp")
    core, x, y, z = place(me)
    mate, x_near, y_near = index_of(1 - core, x, y, z), index_of(core, 1 - x, y, z), index_of(core, x, 1 - y, z)
    half = part_ref.shape[1] // 2
    halves = (pl.ds(0, half), pl.ds(half, half))
    greet(
        [(mate, None), (x_near, None), (y_near, None), (me - 8, z > 0), (me + 8, z < depth - 1)]
    )

    def remote(source, target, send, recv, device):
        return pltpu.make_async_remote_copy(
            src_ref=source, dst_ref=target, send_sem=send, recv_sem=recv, device_id=(device,), device_id_type=MESH
        )

    def level_at(step):
        low, high = jnp.minimum(z, depth - 1 - z), jnp.maximum(z, depth - 1 - z)
        side_up = depth - 1 - z >= z
        single = high - low
        distance_single = high - step
        pair = (step - single) // 2
        distance_pair = low - pair
        first_of_pair = lax.rem(step - single, 2) == 0
        distance = jnp.where(step < single, distance_single, distance_pair)
        up = jnp.where(step < single, side_up, first_of_pair)
        return jnp.where(up, z + distance, z - distance)

    order = [level_at(step) for step in range(depth)]
    def owner(level, slot, which_core):
        return index_of(which_core, 1 - x if slot in (1, 3) else x, 1 - y if slot in (2, 3) else y, level)

    def to_mate(step, slot):
        return remote(
            part_ref.at[owner(order[step], slot, 1 - core)],
            mates.at[step, slot],
            mate_send.at[step, slot],
            mate_recv.at[step, slot],
            mate,
        )

    def load(step, slot):
        return pltpu.make_async_copy(part_ref.at[owner(order[step], slot, core)], held.at[step, slot], load_sem.at[step, slot])

    slots = (3, 1, 2, 0)
    for step in range(depth):
        for slot in slots:
            to_mate(step, slot).start()
            load(step, slot).start()

    tiles = max(t for t in range(1, 17) if half % t == 0)

    def add(target, sources, first, count):
        @pl.loop(0, count // tiles)
        def _(i):
            at = pl.ds(first + i * tiles, tiles)
            total = target[at].astype(jnp.float32)
            for source, shift in sources:
                total = total + source[pl.ds(first - shift + i * tiles, tiles)].astype(jnp.float32)
            target[at] = total.astype(target.dtype)

    def corner_out(step):
        return (
            remote(held.at[step, 3, halves[0]], halfs.at[step, 0], half_send.at[step, 0], half_recv.at[step, 0], y_near),
            remote(held.at[step, 3, halves[1]], halfs.at[step, 1], half_send.at[step, 1], half_recv.at[step, 1], x_near),
        )

    def full_out(step):
        return (
            remote(held.at[step, 1], fulls.at[step, 0], full_send.at[step, 0], full_recv.at[step, 0], x_near),
            remote(held.at[step, 2], fulls.at[step, 1], full_send.at[step, 1], full_recv.at[step, 1], y_near),
        )

    def line_out(step, up):
        level = order[step]
        if up:
            return remote(held.at[step, 0], lines.at[level], line_send.at[step], line_recv.at[level], me + 8)
        slot = jnp.where(level == z - 1, depth, level)
        return remote(held.at[step, 0], lines.at[slot], line_send.at[step], line_recv.at[slot], me - 8)

    def line_in(slot):
        remote(held.at[0, 0], lines.at[slot], line_send.at[0], line_recv.at[slot], me).wait_recv()

    def chip_sum(step, slot):
        to_mate(step, slot).wait_recv()
        load(step, slot).wait()
        add(held.at[step, slot], [(mates.at[step, slot], 0)], 0, 2 * half)

    def begin(step):
        chip_sum(step, 3)
        for c in corner_out(step):
            c.start()
        chip_sum(step, 1)
        chip_sum(step, 2)
        chip_sum(step, 0)

    def middle(step):
        by_y, by_x = corner_out(step)
        by_y.wait_recv()
        add(held.at[step, 1], [(halfs.at[step, 0], 0)], 0, half)
        to_x, to_y = full_out(step)
        to_x.start()
        by_x.wait_recv()
        add(held.at[step, 2], [(halfs.at[step, 1], half)], half, half)
        to_y.start()

    def end(step):
        level = order[step]
        to_x, to_y = full_out(step)
        to_x.wait_recv()
        to_y.wait_recv()
        if step < depth - 1:
            near = [(fulls.at[step, 0], 0), (fulls.at[step, 1], 0)]

            @pl.when(level > z)
            def _():
                @pl.when(z > 0)
                def _():
                    line_in(level)
                    add(held.at[step, 0], near + [(lines.at[level], 0)], 0, 2 * half)

                @pl.when(z == 0)
                def _():
                    add(held.at[step, 0], near, 0, 2 * half)

                line_out(step, True).start()

            @pl.when(level < z)
            def _():
                @pl.when(z < depth - 1)
                def _():
                    line_in(level)
                    add(held.at[step, 0], near + [(lines.at[level], 0)], 0, 2 * half)

                @pl.when(z == depth - 1)
                def _():
                    add(held.at[step, 0], near, 0, 2 * half)

                line_out(step, False).start()

    def total():
        step = depth - 1

        def write(sources):
            @pl.loop(0, 2 * half // tiles)
            def _(i):
                at = pl.ds(i * tiles, tiles)
                value = held[step, 0, at].astype(jnp.float32)
                for source in sources:
                    value = value + source[at].astype(jnp.float32)
                out_ref[at] = value

        near = [fulls.at[step, 0], fulls.at[step, 1]]

        @pl.when(z > 0)
        def _():
            line_in(z)

        @pl.when(z < depth - 1)
        def _():
            line_in(depth)

        @pl.when((z > 0) & (z < depth - 1))
        def _():
            write(near + [lines.at[z], lines.at[depth]])

        @pl.when(z == 0)
        def _():
            write(near + [lines.at[depth]])

        @pl.when(z == depth - 1)
        def _():
            write(near + [lines.at[z]])

    for step in range(depth):
        begin(step)
        if step >= 1:
            middle(step - 1)
        if step >= 2:
            end(step - 2)
    middle(depth - 1)
    end(depth - 2)
    end(depth - 1)
    total()
    for step in range(depth):
        for slot in slots:
            to_mate(step, slot).wait_send()
        for c in corner_out(step) + full_out(step):
            c.wait_send()
        if step < depth - 1:
            line_out(step, True).wait_send()


def scatter_blocks(parts, kernels):
    count, block = parts.shape[:2]
    if not kernels:
        received = lax.all_to_all(parts, "fsdp", split_axis=0, concat_axis=0, tiled=True)
        return jnp.sum(received.astype(jnp.float32), axis=0)
    depth = count // 8
    dma = pltpu.SemaphoreType.DMA
    full, part = (block, ROWS, LANES), (block // 2, ROWS, LANES)
    vmem = lambda lead, shape: pltpu.VMEM((*lead, *shape), parts.dtype)
    return pl.pallas_call(
        functools.partial(scatter_kernel, depth),
        out_shape=jax.ShapeDtypeStruct(full, jnp.float32),
        in_specs=[pl.BlockSpec(memory_space=pl.ANY)],
        out_specs=pl.BlockSpec(memory_space=pltpu.VMEM),
        scratch_shapes=[
            vmem((depth, 4), full), vmem((depth, 4), full), vmem((depth, 2), part), vmem((depth, 2), full), vmem((depth + 1,), full),
            dma((depth, 4)), dma((depth, 4)), dma((depth, 4)), dma((depth, 2)), dma((depth, 2)), dma((depth, 2)), dma((depth, 2)),
            dma((depth,)), dma((depth + 1,)),
        ],
        compiler_params=pltpu.CompilerParams(collective_id=1, has_side_effects=True, vmem_limit_bytes=62 << 20),
        name="scatter_blocks",
    )(parts)


BF = jnp.bfloat16
F32 = jnp.float32
PAIR = 2 * LANES
SCALE = HEAD_DIM**-0.5
GELU_A = math.sqrt(2.0 / math.pi)
GELU_B = 0.044715
ANY = pl.BlockSpec(memory_space=pl.ANY)
VM = pl.BlockSpec(memory_space=pltpu.VMEM)
VMEM_LIMIT = 63 << 20


def nn(left, right):
    return lax.dot_general(left, right, (((1,), (0,)), ((), ())), preferred_element_type=F32)


def nt(left, right):
    return lax.dot_general(left, right, (((1,), (1,)), ((), ())), preferred_element_type=F32)


def runs_of(where, name):
    runs, done = [], 0
    for owner, at, tiles in where[name]:
        if runs and runs[-1][0] == owner and runs[-1][1] + runs[-1][2] == at:
            runs[-1][2] += tiles
        else:
            runs.append([owner, at, tiles, done])
        done += tiles
    return runs


def copies(where, name, blocks_ref, tiles_ref, sem, out=False):
    made = []
    flat_tiles = tiles_ref if len(tiles_ref.shape) == 3 else tiles_ref.reshape(-1, ROWS, LANES)
    for owner, at, tiles, done in runs_of(where, name):
        there, here = blocks_ref.at[owner, pl.ds(at, tiles)], flat_tiles.at[pl.ds(done, tiles)]
        made.append(pltpu.make_async_copy(here, there, sem) if out else pltpu.make_async_copy(there, here, sem))
    return made


def start(made):
    for copy in made:
        copy.start()


def wait(made):
    for copy in made:
        copy.wait()


def panel(tiles_ref, c, units, first=0):
    return tiles_ref[pl.ds(first, units), pl.ds(c, 1)].reshape(units * ROWS, LANES)


def panels(tiles_ref, c, many, units, first=0):
    return jnp.concatenate([panel(tiles_ref, c + i, units, first) for i in range(many)], axis=1)


def put_panel(tiles_ref, c, value, first=0):
    units = value.shape[0] // ROWS
    tiles_ref[pl.ds(first, units), pl.ds(c, 1)] = value.astype(BF).reshape(units, 1, ROWS, LANES)


def put_panels(tiles_ref, c, value, first=0):
    for i in range(value.shape[1] // LANES):
        put_panel(tiles_ref, c + i, value[:, i * LANES : (i + 1) * LANES], first)


def vector_rows(tiles_ref):
    return jnp.concatenate([tiles_ref[i].astype(F32) for i in range(tiles_ref.shape[0])], axis=0)


def as_row(rows, first, many):
    return jnp.concatenate([rows[first + i : first + i + 1] for i in range(many)], axis=1)


def put_vectors(tiles_ref, rows_list):
    parts = [row[:, i * LANES : (i + 1) * LANES] for row in rows_list for i in range(row.shape[1] // LANES)]
    missing = tiles_ref.shape[0] * ROWS - len(parts)
    whole = jnp.concatenate(parts + [jnp.zeros((missing, LANES), F32)] if missing else parts, axis=0)
    for i in range(tiles_ref.shape[0]):
        tiles_ref[i] = whole[i * ROWS : (i + 1) * ROWS].astype(BF)


def norm_rows(values):
    centre = values - jnp.mean(values, axis=-1, keepdims=True)
    inverse = lax.rsqrt(jnp.mean(centre * centre, axis=-1, keepdims=True) + EPS)
    return centre * inverse, inverse


def norm_rows_back(grad, normed, inverse, gain):
    scaled = grad * gain
    return inverse * (
        scaled - jnp.mean(scaled, axis=-1, keepdims=True) - normed * jnp.mean(scaled * normed, axis=-1, keepdims=True)
    )


def column_sums(values):
    return jnp.sum(values, axis=0, keepdims=True)


def head_window(h):
    block = jnp.minimum((h * HEAD_DIM) // LANES, DC - 2)
    lane = pl.multiple_of(block * LANES, LANES)
    return lane, h * HEAD_DIM - lane


def head_mask(rows, offset):
    lane = lax.broadcasted_iota(jnp.int32, (rows, PAIR), 1)
    return (lane >= offset) & (lane < offset + HEAD_DIM)


def front_kernel(
    where, x_ref, segq_ref, segk_ref, blocks_ref, q_ref, k_ref, v_ref, attended_ref, logs_ref,
    normed_ref, w_ref, vec1_ref, vec2_ref, bias_ref, score_ref, prob_ref, sem, vec_sem,
):
    window, rows = x_ref.shape[0], q_ref.shape[0]
    margin = (window - rows) // 2
    loads = [copies(where, name, blocks_ref, w_ref.at[i], sem.at[i]) for i, name in enumerate(("w_query", "w_key", "w_value"))]
    vecs = copies(where, "vec1", blocks_ref, vec1_ref, vec_sem) + copies(where, "vec2", blocks_ref, vec2_ref, vec_sem)
    start(vecs)
    for made in loads:
        start(made)
    wait(vecs)
    vec = vector_rows(vec1_ref)
    gain, shift = as_row(vec, 0, DC), as_row(vec, DC, DC)
    step = rows // 3

    @pl.loop(0, window // step)
    def _(i):
        at = pl.ds(i * step, step)
        normed, _ = norm_rows(x_ref[at].astype(F32))
        normed_ref[at] = (normed * gain + shift).astype(BF)

    @pl.loop(0, rows // 8)
    def _(i):
        at = pl.ds(i * 8, 8)
        bias_ref[at] = jnp.where(segq_ref[at] == segk_ref[...], 0.0, NEG)

    biases = vector_rows(vec2_ref)
    zero = jnp.zeros((1, D), F32)
    for made in loads:
        wait(made)
    for i, (out, add) in enumerate(((q_ref, as_row(biases, 0, DC)), (k_ref, zero), (v_ref, as_row(biases, DC, DC)))):
        for c in range(0, DC, 2):
            many = min(2, DC - c)
            lanes = slice(c * LANES, (c + many) * LANES)
            weights = panels(w_ref.at[i], c, many, D // ROWS)
            if i == 0:
                out[:, lanes] = (nn(normed_ref[pl.ds(margin, rows)], weights) + add[:, lanes]).astype(BF)
            else:

                @pl.loop(0, window // rows)
                def _(b):
                    at = pl.ds(b * rows, rows)
                    out[at, lanes] = (nn(normed_ref[at], weights) + add[:, lanes]).astype(BF)

    attended_ref[...] = jnp.zeros_like(attended_ref)
    logs_ref[...] = jnp.zeros_like(logs_ref)
    lane_l = lax.broadcasted_iota(jnp.int32, logs_ref.shape, 1)

    @pl.loop(0, HEADS)
    def _(h):
        lane, offset = head_window(h)
        mask = head_mask(rows, offset)
        lanes = pl.ds(lane, PAIR)
        query = jnp.where(mask, q_ref[:, lanes], jnp.zeros((), BF))
        score_ref[...] = nt(query, k_ref[:, lanes]) * SCALE + bias_ref[...]
        top = jnp.max(score_ref[...], axis=-1, keepdims=True)
        powers = jnp.exp(score_ref[...] - top)
        total = jnp.sum(powers, axis=-1, keepdims=True)
        prob_ref[...] = powers.astype(BF)
        out = nn(prob_ref[...], v_ref[:, lanes]) / total
        attended_ref[:, lanes] = jnp.where(mask, out.astype(BF), attended_ref[:, lanes])
        logs_ref[...] = jnp.where(lane_l == h, top + jnp.log(total), logs_ref[...])


def front(x_win, seg_query, seg_keys, gathered, where, rows):
    window = x_win.shape[0]
    shape = lambda n, d=D, t=BF: jax.ShapeDtypeStruct((n, d), t)
    dma = pltpu.SemaphoreType.DMA
    units = D // ROWS
    return pl.pallas_call(
        functools.partial(front_kernel, where),
        out_shape=(shape(rows), shape(window), shape(window), shape(rows), shape(rows, LANES, F32)),
        in_specs=[VM, VM, VM, ANY],
        out_specs=[VM] * 5,
        scratch_shapes=[
            pltpu.VMEM((window, D), BF),
            pltpu.VMEM((3, units, DC, ROWS, LANES), BF), pltpu.VMEM((2, ROWS, LANES), BF), pltpu.VMEM((2, ROWS, LANES), BF),
            pltpu.VMEM((rows, window), F32), pltpu.VMEM((rows, window), F32), pltpu.VMEM((rows, window), BF), dma((3,)), dma,
        ],
        compiler_params=pltpu.CompilerParams(vmem_limit_bytes=VMEM_LIMIT),
        name="front",
    )(x_win, seg_query, seg_keys, gathered)


def middle_kernel(
    where, x_ref, cot_ref, attended_ref, blocks_ref, act_ref, mid_grad_ref, att_grad_ref, parts_ref,
    wo_ref, wu_ref, wd_ref, vec3_ref, vec4_ref, vec5_ref, b_up_ref, hidden_ref, slope_ref, pre_ref, normed_ref, normed_b_ref,
    mid_ref, g_up_ref, sem, out_sem,
):
    rows = x_ref.shape[0]
    units, f_units = D // ROWS, FF // ROWS
    names = ("w_out", "w_up", "w_down", "vec3", "vec4", "vec5")
    refs = (wo_ref, wu_ref, wd_ref, vec3_ref, vec4_ref, vec5_ref)
    loads = {n: copies(where, n, blocks_ref, r, sem.at[i]) for i, (n, r) in enumerate(zip(names, refs))}
    saves = {n: copies(where, n, parts_ref, r, out_sem, out=True) for n, r in zip(names, refs)}
    for n in ("vec3", "vec4", "vec5", "w_out", "w_up", "w_down"):
        start(loads[n])
    f_wide = FC * LANES
    pads = f_wide // ROWS - f_units
    wd_ref[pl.ds(f_units, pads)] = jnp.zeros((pads, DC, ROWS, LANES), BF)
    for n in ("vec3", "vec4", "vec5", "w_out"):
        wait(loads[n])
    vec = vector_rows(vec3_ref)
    b_out, gain, shift = (as_row(vec, i * DC, DC) for i in range(3))
    vec = vector_rows(vec4_ref)
    entry = lax.broadcasted_iota(jnp.int32, vec.shape, 0) * LANES + lax.broadcasted_iota(jnp.int32, vec.shape, 1)
    b_up_ref[...] = jnp.where(entry < FF, vec, 0.0)
    b_down = jnp.concatenate([vec5_ref[c].astype(F32)[0:1] for c in range(DC)], axis=1)

    for c in range(0, DC, 2):
        many = min(2, DC - c)
        lanes = slice(c * LANES, (c + many) * LANES)
        mid_ref[:, lanes] = (
            x_ref[:, lanes].astype(F32) + nn(attended_ref[...], panels(wo_ref, c, many, units)) + b_out[:, lanes]
        )
    normed, inverse = norm_rows(mid_ref[...])
    normed_ref[...] = normed
    normed_b_ref[...] = (normed * gain + shift).astype(BF)

    wait(loads["w_up"])

    @pl.loop(0, FC // 2)
    def _(p):
        at = pl.ds(pl.multiple_of(p * PAIR, PAIR), PAIR)
        bias = jnp.concatenate([b_up_ref[pl.ds(2 * p, 1)], b_up_ref[pl.ds(2 * p + 1, 1)]], axis=1)
        v = nn(normed_b_ref[...], panels(wu_ref, 2 * p, 2, units)) + bias
        square = v * v
        bent = jnp.tanh(GELU_A * v * (1.0 + GELU_B * square))
        hidden_ref[:, at] = (0.5 * v * (1.0 + bent)).astype(BF)
        slope_ref[:, at] = 0.5 * (1.0 + bent) + 0.5 * v * (1.0 - bent * bent) * (
            GELU_A * (1.0 + 3.0 * GELU_B * square)
        )

    wait(loads["w_down"])
    for c in range(0, DC, 2):
        many = min(2, DC - c)
        lanes = slice(c * LANES, (c + many) * LANES)
        act_ref[:, lanes] = (
            mid_ref[:, lanes] + nn(hidden_ref[...], panels(wd_ref, c, many, f_wide // ROWS)) + b_down[:, lanes]
        ).astype(BF)

    @pl.loop(0, FC // 2)
    def _(p):
        at = pl.ds(pl.multiple_of(p * PAIR, PAIR), PAIR)
        first = p * (PAIR // ROWS)
        grad = nt(cot_ref[...], panels(wd_ref, 0, DC, PAIR // ROWS, first)) * slope_ref[:, at]
        pre_ref[:, at] = grad.astype(BF)
        sums = column_sums(grad)
        g_up_ref[pl.ds(2 * p, 1)] = sums[:, :LANES]
        g_up_ref[pl.ds(2 * p + 1, 1)] = sums[:, LANES:]
        put_panels(wd_ref, 0, nn(hidden_ref[:, at].T, cot_ref[...]), first)

    start(saves["w_down"])
    put_vectors(vec4_ref, [b_up_row for b_up_row in [g_up_ref[i : i + 1] for i in range(FC)]])
    start(saves["vec4"])
    cot = cot_ref[...].astype(F32)
    sums = column_sums(cot)
    row0 = lax.broadcasted_iota(jnp.int32, (ROWS, LANES), 0) == 0
    for c in range(DC):
        vec5_ref[c] = jnp.where(row0, sums[:, c * LANES : (c + 1) * LANES], 0.0).astype(BF)
    start(saves["vec5"])

    for c in range(0, DC, 2):
        many = min(2, DC - c)
        weights = panels(wu_ref, 0, FC, many * LANES // ROWS, c * LANES // ROWS)
        mid_ref[:, c * LANES : (c + many) * LANES] = nt(pre_ref[...], weights)
    e = mid_ref[...]
    normed = normed_ref[...]
    g_gain, g_shift = column_sums(e * normed), column_sums(e)
    mid_grad = cot + norm_rows_back(e, normed, inverse, gain)
    mid_grad_ref[...] = mid_grad
    put_vectors(vec3_ref, [column_sums(mid_grad), g_gain, g_shift])
    start(saves["vec3"])
    mid_b = mid_grad.astype(BF)
    for c in range(0, DC, 2):
        many = min(2, DC - c)
        lanes = slice(c * LANES, (c + many) * LANES)
        weights = panels(wo_ref, 0, DC, many * LANES // ROWS, c * LANES // ROWS)
        att_grad_ref[:, lanes] = nt(mid_b, weights).astype(BF)
    turned = attended_ref[...].T
    for c in range(0, DC, 2):
        many = min(2, DC - c)
        put_panels(wo_ref, c, nn(turned, mid_b[:, c * LANES : (c + many) * LANES]))
    start(saves["w_out"])
    turned_b = normed_b_ref[...].T

    @pl.loop(0, FC // 2)
    def _(p):
        at = pl.ds(pl.multiple_of(p * PAIR, PAIR), PAIR)
        put_panels(wu_ref, 2 * p, nn(turned_b, pre_ref[:, at]))

    start(saves["w_up"])
    for n in names:
        wait(saves[n])


def middle(block_input, cotangent, attended, gathered, where):
    rows = block_input.shape[0]
    shape = lambda t: jax.ShapeDtypeStruct((rows, D), t)
    dma = pltpu.SemaphoreType.DMA
    tiles = lambda *n: pltpu.VMEM((*n, ROWS, LANES), BF)
    units, f_wide = D // ROWS, FC * LANES
    return pl.pallas_call(
        functools.partial(middle_kernel, where),
        out_shape=(shape(BF), shape(F32), shape(BF), jax.ShapeDtypeStruct(gathered.shape, BF)),
        in_specs=[VM, VM, VM, ANY],
        out_specs=[VM, VM, VM, ANY],
        scratch_shapes=[
            tiles(units, DC), tiles(units, FC), tiles(f_wide // ROWS, DC), tiles(2), tiles(3), tiles(DC),
            pltpu.VMEM((3 * ROWS, LANES), F32), pltpu.VMEM((rows, f_wide), BF), pltpu.VMEM((rows, f_wide), F32),
            pltpu.VMEM((rows, f_wide), BF), pltpu.VMEM((rows, D), F32), pltpu.VMEM((rows, D), BF), pltpu.VMEM((rows, D), F32),
            pltpu.VMEM((3 * ROWS, LANES), F32), dma((6,)), dma,
        ],
        compiler_params=pltpu.CompilerParams(vmem_limit_bytes=VMEM_LIMIT),
        name="middle",
    )(block_input, cotangent, attended, gathered)


def back_kernel(
    where, x_hbm_ref, segq_ref, segk_ref, blocks_ref, q_ref, k_ref, v_ref, grad_ref, logs_ref, parts_in_ref,
    near_ref, own_ref, parts_ref,
    w_ref, vec1_ref, vec2_ref, bias_ref, score_ref, prob_ref, turned_ref, dk_ref, dv_ref, dq_ref, part_ref, logs_t_ref, x_ref,
    sem, vec_sem, out_sem, x_sem,
):
    window, rows = x_ref.shape[0], q_ref.shape[0]
    margin = (window - rows) // 2
    units = D // ROWS
    names = ("w_query", "w_key", "w_value")
    loads = [copies(where, name, blocks_ref, w_ref.at[i], sem.at[i]) for i, name in enumerate(names)]
    vecs = copies(where, "vec1", blocks_ref, vec1_ref, vec_sem)
    start(vecs)
    for made in loads:
        start(made)
    x_load = pltpu.make_async_copy(x_hbm_ref, x_ref, x_sem)
    x_load.start()

    @pl.loop(0, window // LANES)
    def _(i):
        at = pl.ds(pl.multiple_of(i * LANES, LANES), LANES)
        bias_ref[at] = jnp.where(segk_ref[at] == segq_ref[...], 0.0, NEG)
        turned_ref[:, at] = k_ref[at].T
        dk_ref[at] = jnp.zeros((LANES, D), F32)
        dv_ref[at] = jnp.zeros((LANES, D), F32)

    logs_t_ref[...] = logs_ref[...].T

    @pl.loop(0, HEADS)
    def _(h):
        lane, offset = head_window(h)
        mask = head_mask(rows, offset)
        lanes = pl.ds(lane, PAIR)
        query = jnp.where(mask, q_ref[:, lanes], jnp.zeros((), BF))
        grad = jnp.where(mask, grad_ref[:, lanes], jnp.zeros((), BF))
        probs = jnp.exp(nt(k_ref[:, lanes], query) * SCALE + bias_ref[...] - logs_t_ref[pl.ds(h, 1)])
        score_ref[...] = probs
        prob_ref[...] = probs.astype(BF)
        prob_grad = nt(v_ref[:, lanes], grad)
        row_total = jnp.sum(score_ref[...] * prob_grad, axis=0, keepdims=True)
        dv_ref[:, lanes] += nn(prob_ref[...], grad)
        prob_ref[...] = (score_ref[...] * (prob_grad - row_total)).astype(BF)
        dk_ref[:, lanes] += nn(prob_ref[...], query)
        part_ref[...] = nn(turned_ref[lanes], prob_ref[...])
        at = pl.ds(pl.multiple_of(h * HEAD_DIM, 8), HEAD_DIM)
        dq_ref[at] = part_ref[pl.ds(pl.multiple_of(offset, 8), HEAD_DIM)]

    dq = dq_ref[...].T * SCALE
    g_query = column_sums(dq)
    dq_b = dq.astype(BF)
    wait(vecs)
    vec = vector_rows(vec1_ref)
    gain, shift = as_row(vec, 0, DC), as_row(vec, DC, DC)
    dk_b_ref, dv_b_ref = k_ref, v_ref
    x_load.wait()
    g_value = jnp.zeros((1, D), F32)
    step = rows // 3

    def rounded(i, total):
        at = pl.ds(pl.multiple_of(i * step, step), step)
        dk_b_ref[at] = (dk_ref[at] * SCALE).astype(BF)
        dv = dv_ref[at]
        dv_b_ref[at] = dv.astype(BF)
        normed, _ = norm_rows(x_ref[at].astype(F32))
        turned_ref[:, at] = (normed * gain + shift).astype(BF).T
        return total + column_sums(dv)

    g_value = lax.fori_loop(0, window // step, rounded, g_value)
    put_vectors(vec2_ref, [g_query, g_value])
    save = copies(where, "vec2", parts_ref, vec2_ref, out_sem, out=True)
    for made in loads:
        wait(made)
    for c in range(0, DC, 2):
        many = min(2, DC - c)
        lanes = slice(c * LANES, (c + many) * LANES)
        part = [panels(w_ref.at[i], 0, DC, many * LANES // ROWS, c * LANES // ROWS) for i in range(3)]

        @pl.loop(0, window // rows)
        def _(b):
            at = pl.ds(b * rows, rows)
            dk_ref[at, lanes] = nt(dk_b_ref[at], part[1]) + nt(dv_b_ref[at], part[2])

        dk_ref[pl.ds(margin, rows), lanes] += nt(dq_b, part[0])
    turned_own = turned_ref[:, pl.ds(margin, rows)]
    for c in range(0, DC, 2):
        many = min(2, DC - c)
        lanes = slice(c * LANES, (c + many) * LANES)
        put_panels(w_ref.at[0], c, nn(turned_own, dq_b[:, lanes]))
        put_panels(w_ref.at[1], c, nn(turned_ref[...], dk_b_ref[:, lanes]))
        put_panels(w_ref.at[2], c, nn(turned_ref[...], dv_b_ref[:, lanes]))
    for i, name in enumerate(names):
        save = save + copies(where, name, parts_ref, w_ref.at[i], out_sem, out=True)
    start(save)

    def norm_block(i, totals):
        at = pl.ds(pl.multiple_of(i * step, step), step)
        normed, inverse = norm_rows(x_ref[at].astype(F32))
        e = dk_ref[at]
        part = norm_rows_back(e, normed, inverse, gain)
        x_ref[at] = part.astype(BF)

        @pl.when((i >= margin // step) & (i < (margin + rows) // step))
        def _():
            own_ref[pl.ds(pl.multiple_of(i * step - margin, step), step)] = part

        return totals[0] + column_sums(e * normed), totals[1] + column_sums(e)

    zero = jnp.zeros((1, D), F32)
    g_gain, g_shift = lax.fori_loop(0, window // step, norm_block, (zero, zero))
    put_vectors(vec1_ref, [g_gain, g_shift])
    last = copies(where, "vec1", parts_ref, vec1_ref, out_sem, out=True)
    last = last + [pltpu.make_async_copy(x_ref, near_ref, x_sem)]
    start(last)
    wait(save + last)


def back(x_win, seg_query, seg_keys, gathered, queries, key_win, value_win, att_grad, logs, parts, where):
    window, rows = x_win.shape[0], queries.shape[0]
    dma = pltpu.SemaphoreType.DMA
    tiles = lambda *n: pltpu.VMEM((*n, ROWS, LANES), BF)
    vm = lambda a, b, t: pltpu.VMEM((a, b), t)
    return pl.pallas_call(
        functools.partial(back_kernel, where),
        out_shape=(
            jax.ShapeDtypeStruct((window, D), BF), jax.ShapeDtypeStruct((rows, D), F32), jax.ShapeDtypeStruct(parts.shape, BF),
        ),
        in_specs=[ANY, VM, VM, ANY, VM, VM, VM, VM, VM, ANY],
        out_specs=[ANY, VM, ANY],
        scratch_shapes=[
            tiles(3, D // ROWS, DC), tiles(2), tiles(2), vm(window, rows, F32), vm(window, rows, F32), vm(window, rows, BF),
            vm(D, window, BF), vm(window, D, F32), vm(window, D, F32), vm(D, rows, F32), vm(PAIR, rows, F32), vm(LANES, rows, F32),
            vm(window, D, BF), dma((3,)), dma, dma, dma,
        ],
        input_output_aliases={9: 2},
        compiler_params=pltpu.CompilerParams(vmem_limit_bytes=VMEM_LIMIT),
        name="back",
    )(x_win, seg_query, seg_keys, gathered, queries, key_win, value_win, att_grad, logs, parts)


HOT_NAMES = ("vec1", "w_query", "w_key", "w_value", "vec2")


def transfer_pieces(plan, depth):
    where, block = plan[:2]
    count = plan[2].shape[0]
    hot = [0] * depth
    for name in HOT_NAMES:
        for owner, at, tiles in where[name]:
            level = owner * depth // count
            hot[level] = max(hot[level], at + tiles)
    hot = [min(block, h + h % 2) for h in hot]
    early = [(level, 0, h) for level, h in enumerate(hot) if h]
    late = [(level, h, block - h) for level, h in enumerate(hot) if h < block]
    return early, late


def cut(piece, many):
    level, first, tiles = piece
    edges = [tiles // 2 * i // (many // 2) if i <= many // 2 else 0 for i in range(many // 2 + 1)]
    half = tiles // 2
    edges = [half * i // (many // 2) for i in range(many // 2)] + [
        half + (tiles - half) * i // (many // 2) for i in range(many // 2 + 1)
    ]
    return [(level, first + a, b - a) for a, b in zip(edges[:-1], edges[1:])]


def gather_front_kernel(
    depth, where, early, late,
    block_ref, x_in_ref, segq_ref, segk_ref,
    out_ref, x_out_ref, x_got_ref, q_ref, k_ref, v_ref, attended_ref, logs_ref,
    z_send, z_recv, x_send, x_recv, y_send, y_recv, corner_send, corner_recv, mate_send, mate_recv, w_send, w_recv,
    local_sem, stage_ref, x_ref, normed_ref, w_ref, vec1_ref, vec2_ref, bias_ref, score_ref, prob_ref, sem, vec_sem,
):
    me = lax.axis_index("fsdp")
    count = 8 * depth
    core, x, y, z = place(me)
    mate, x_near, y_near = index_of(1 - core, x, y, z), index_of(core, 1 - x, y, z), index_of(core, x, 1 - y, z)
    up, down = me + 8, me - 8
    after, before = me + 2, me - 2
    has_after, has_before = after < count, before >= 0
    greet(
        [(mate, None), (x_near, None), (y_near, None), (down, z > 0), (up, z < depth - 1), (after, has_after), (before, has_before)]
    )
    pieces = early + late
    chunks = {p: cut(piece, 4) if piece[0] == 0 and p < len(early) else [piece] for p, piece in enumerate(pieces)}
    chunk_list = [(p, chunk) for p in chunks for chunk in chunks[p]]
    ids = {p: [i for i, (q, _) in enumerate(chunk_list) if q == p] for p in chunks}
    hot, cold = range(len(early)), range(len(early), len(pieces))

    def remote(source, target, send, recv, device):
        return pltpu.make_async_remote_copy(
            src_ref=source, dst_ref=target, send_sem=send, recv_sem=recv, device_id=(device,), device_id_type=MESH
        )

    def span(piece):
        return pl.ds(piece[1], piece[2])

    def halves(p):
        level, first, tiles = pieces[p]
        return (level, first, tiles // 2), (level, first + tiles // 2, tiles - tiles // 2)

    def column(level):
        return index_of(core, x, y, level)

    def from_x(level):
        return index_of(core, 1 - x, y, level)

    def from_y(level):
        return index_of(core, x, 1 - y, level)

    def across(level):
        return index_of(core, 1 - x, 1 - y, level)

    def pass_on(block, piece, send, recv, device, own=False):
        there = out_ref.at[block, span(piece)]
        return remote(block_ref.at[span(piece)] if own else there, there, send, recv, device)

    def z_copy(i, upward, own=False):
        piece = chunk_list[i][1]
        return pass_on(column(piece[0]), piece, z_send.at[i, 0 if upward else 1], z_recv.at[i], up if upward else down, own)

    def plane_copies(i, own=False):
        piece = chunk_list[i][1]
        block = column(piece[0])
        return (
            pass_on(block, piece, x_send.at[i], x_recv.at[i], x_near, own),
            pass_on(block, piece, y_send.at[i], y_recv.at[i], y_near, own),
            pass_on(block, piece, mate_send.at[0, i], mate_recv.at[0, i], mate, own),
        )

    def got(block, i, recv):
        piece = chunk_list[i][1]
        pass_on(block, piece, x_send.at[i], recv, me).wait_recv()

    def spread(i, own=False):
        for copy in plane_copies(i, own):
            copy.start()

    def take(i):
        def run(zv):
            level = chunk_list[i][1][0]
            got(column(level), i, z_recv.at[i])
            if level < zv < depth - 1:
                z_copy(i, True).start()
            if 0 < zv < level:
                z_copy(i, False).start()
            spread(i)

        return run

    def corner_copies(p):
        level = pieces[p][0]
        first, second = halves(p)
        return (
            pass_on(from_x(level), first, corner_send.at[p, 0], corner_recv.at[p, 0], y_near),
            pass_on(from_y(level), second, corner_send.at[p, 1], corner_recv.at[p, 1], x_near),
        )

    def mate_copies(p):
        level = pieces[p][0]
        first, second = halves(p)
        return (
            pass_on(from_x(level), pieces[p], mate_send.at[1, p], mate_recv.at[1, p], mate),
            pass_on(from_y(level), pieces[p], mate_send.at[2, p], mate_recv.at[2, p], mate),
            pass_on(across(level), first, mate_send.at[3, p], mate_recv.at[3, p], mate),
            pass_on(across(level), second, mate_send.at[4, p], mate_recv.at[4, p], mate),
        )

    def beside(p):
        def run(zv):
            level = pieces[p][0]
            for i in ids[p]:
                got(from_x(level), i, x_recv.at[i])
            corner_copies(p)[0].start()
            mate_copies(p)[0].start()
            for i in ids[p]:
                got(from_y(level), i, y_recv.at[i])
            corner_copies(p)[1].start()
            mate_copies(p)[1].start()

        return run

    def corner(p):
        def run(zv):
            level = pieces[p][0]
            for side, half in enumerate(halves(p)):
                pass_on(across(level), half, corner_send.at[p, side], corner_recv.at[p, side], me).wait_recv()
                mate_copies(p)[2 + side].start()

        return run

    def from_mate(p):
        def run(zv):
            level = pieces[p][0]
            other = 1 - 2 * core
            for i in ids[p]:
                pass_on(column(level) + other, chunk_list[i][1], mate_send.at[0, i], mate_recv.at[0, i], me).wait_recv()
            first, second = halves(p)
            for slot, (block, piece) in enumerate(
                ((from_x(level), pieces[p]), (from_y(level), pieces[p]), (across(level), first), (across(level), second))
            ):
                pass_on(block + other, piece, mate_send.at[slot + 1, p], mate_recv.at[slot + 1, p], me).wait_recv()

        return run

    def own_spread(i):
        return lambda zv: spread(i, True)

    def own_up(i):
        return lambda zv: z_copy(i, True, True).start() if zv < depth - 1 else None

    def own_down(i):
        return lambda zv: z_copy(i, False, True).start() if zv > 0 else None

    def w_copy(slot, which, device, source=None):
        return remote(x_in_ref if source is None else source, x_got_ref.at[slot], w_send.at[which], w_recv.at[slot], device)

    def w_start():
        w_copy(1 + 2 * core, 0, mate).start()

        @pl.when(has_after)
        def _():
            w_copy(0, 1, after).start()

        @pl.when(has_before)
        def _():
            w_copy(4, 2, before).start()

    def w_forward(core_index):
        slot = 0 if core_index else 4
        return w_copy(1 if core_index else 3, 3, mate, x_got_ref.at[slot])

    def w_wait(slot):
        w_copy(slot, 0, me).wait_recv()

    def w_middle(zv):
        @pl.when(has_before)
        def _():
            w_wait(0)

        @pl.when(has_after)
        def _():
            w_wait(4)

        @pl.when((core == 1) & has_before)
        def _():
            w_forward(1).start()

        @pl.when((core == 0) & has_after)
        def _():
            w_forward(0).start()

    first_cold = {0: 0, 1: 0, 2: 1, 3: 2}
    levels = [pieces[p][0] for p in cold]

    def lists(zv):
        own_hot = [p for p in hot if pieces[p][0] == zv]
        own_cold = [p for p in cold if pieces[p][0] == zv]
        far_hot = sorted((p for p in hot if pieces[p][0] != zv), key=lambda p: abs(pieces[p][0] - zv))
        far_cold = sorted((p for p in cold if pieces[p][0] != zv), key=lambda p: (abs(pieces[p][0] - zv), -pieces[p][0]))
        start = []
        for p in own_hot:
            for i in ids[p]:
                start += [own_up(i), own_down(i), own_spread(i)]
        for p in own_cold:
            start += [own_down(i) for i in ids[p]]
        for p in far_hot:
            start += [take(i) for i in ids[p]]
        for p in own_cold:
            start += [own_up(i) for i in ids[p]]
        start.append(w_middle)
        order_hot = own_hot + far_hot
        start += [beside(p) for p in order_hot]
        for p in own_cold:
            start += [own_spread(i) for i in ids[p]]
        near = [p for p in far_cold if abs(pieces[p][0] - zv) == 1]
        rest = [p for p in far_cold if p not in near]
        for p in near:
            start += [take(i) for i in ids[p]]
        start += [corner(p) for p in order_hot]
        start += [from_mate(p) for p in order_hot]
        return start, [[take(i) for p in rest for i in ids[p]], own_cold + near + rest]

    plans = [lists(zv) for zv in range(depth)]

    def each_plane(events_of):
        for zv in range(depth):
            events = events_of(zv)
            if events:

                @pl.when(z == zv)
                def _():
                    for event in events:
                        event(zv)

    w_start()
    fill = pltpu.make_async_copy(block_ref, stage_ref, local_sem)
    fill.start()
    fill.wait()
    keep = pltpu.make_async_copy(stage_ref, out_ref.at[me], local_sem)
    keep.start()
    each_plane(lambda zv: plans[zv][0])
    keep.wait()

    def cold_step(k, step):
        return lambda zv: [step(plans[zv][1][1][k])] if k < len(plans[zv][1][1]) else []

    services = {
        "takes": lambda zv: plans[zv][1][0],
        **{("beside", k): cold_step(k, beside) for k in range(len(cold))},
        **{("corner", k): cold_step(k, corner) for k in range(len(cold))},
    }

    def service(name):
        each_plane(services[name])

    rows = q_ref.shape[0]
    window = k_ref.shape[0]
    margin = (window - rows) // 2
    w_wait(3 - 2 * core)

    @pl.when((core == 0) & has_before)
    def _():
        w_wait(1)

    @pl.when((core == 1) & has_after)
    def _():
        w_wait(3)

    near_sem = vec_sem
    present = (before >= 0, (core == 1) | has_before, None, (core == 0) | has_after, after < count)
    for slot, there in enumerate(present):
        at = x_ref.at[pl.ds(slot * rows, rows)]
        if there is None:
            pltpu.make_async_copy(x_in_ref, at, near_sem).start()
            continue

        @pl.when(there)
        def _():
            pltpu.make_async_copy(x_got_ref.at[slot], at, near_sem).start()

        @pl.when(jnp.logical_not(there))
        def _():
            pltpu.make_async_copy(x_in_ref, at, near_sem).start()

    for slot in range(5):
        pltpu.make_async_copy(x_in_ref, x_ref.at[pl.ds(slot * rows, rows)], near_sem).wait()
    x_save = pltpu.make_async_copy(x_ref, x_out_ref, local_sem)
    x_save.start()
    loads = [copies(where, name, out_ref, w_ref.at[i], sem.at[i]) for i, name in enumerate(("w_query", "w_key", "w_value"))]
    vecs = copies(where, "vec1", out_ref, vec1_ref, vec_sem) + copies(where, "vec2", out_ref, vec2_ref, vec_sem)
    start(vecs)
    for made in loads:
        start(made)
    wait(vecs)
    vec = vector_rows(vec1_ref)
    gain, shift = as_row(vec, 0, DC), as_row(vec, DC, DC)
    step = rows // 3

    @pl.loop(0, window // step)
    def _(i):
        at = pl.ds(i * step, step)
        normed, _ = norm_rows(x_ref[at].astype(F32))
        normed_ref[at] = (normed * gain + shift).astype(BF)

    @pl.loop(0, rows // 8)
    def _(i):
        at = pl.ds(i * 8, 8)
        bias_ref[at] = jnp.where(segq_ref[at] == segk_ref[...], 0.0, NEG)

    biases = vector_rows(vec2_ref)
    zero = jnp.zeros((1, D), F32)
    for made in loads:
        wait(made)
    for i, (out, add) in enumerate(((q_ref, as_row(biases, 0, DC)), (k_ref, zero), (v_ref, as_row(biases, DC, DC)))):
        for c in range(0, DC, 2):
            many = min(2, DC - c)
            lanes = slice(c * LANES, (c + many) * LANES)
            weights = panels(w_ref.at[i], c, many, D // ROWS)
            if i == 0:
                out[:, lanes] = (nn(normed_ref[pl.ds(margin, rows)], weights) + add[:, lanes]).astype(BF)
            else:

                @pl.loop(0, window // rows)
                def _(b):
                    at = pl.ds(b * rows, rows)
                    out[at, lanes] = (nn(normed_ref[at], weights) + add[:, lanes]).astype(BF)

        if i == 1:
            service("takes")
    attended_ref[...] = jnp.zeros_like(attended_ref)
    logs_ref[...] = jnp.zeros_like(logs_ref)
    lane_l = lax.broadcasted_iota(jnp.int32, logs_ref.shape, 1)
    when = {("beside", k): (0, 4, 10)[min(k, 2)] for k in range(len(cold))}
    when |= {("corner", k): (12, 15, 16)[min(k, 2)] for k in range(len(cold))}

    @pl.loop(0, HEADS)
    def _(h):
        for name, at_head in when.items():
            if at_head < HEADS:

                @pl.when(h == at_head)
                def _():
                    service(name)

        lane, offset = head_window(h)
        mask = head_mask(rows, offset)
        lanes = pl.ds(lane, PAIR)
        query = jnp.where(mask, q_ref[:, lanes], jnp.zeros((), BF))
        score_ref[...] = nt(query, k_ref[:, lanes]) * SCALE + bias_ref[...]
        top = jnp.max(score_ref[...], axis=-1, keepdims=True)
        powers = jnp.exp(score_ref[...] - top)
        total = jnp.sum(powers, axis=-1, keepdims=True)
        prob_ref[...] = powers.astype(BF)
        out = nn(prob_ref[...], v_ref[:, lanes]) / total
        attended_ref[:, lanes] = jnp.where(mask, out.astype(BF), attended_ref[:, lanes])
        logs_ref[...] = jnp.where(lane_l == h, top + jnp.log(total), logs_ref[...])

    for name, at_head in when.items():
        if at_head >= HEADS:
            service(name)
    each_plane(lambda zv: [from_mate(p) for p in plans[zv][1][1]])

    def sent(zv):
        for i, (p, piece) in enumerate(chunk_list):
            for copy in plane_copies(i):
                copy.wait_send()
            level = piece[0]
            if zv < depth - 1 and level <= zv:
                z_copy(i, True).wait_send()
            if zv > 0 and level >= zv:
                z_copy(i, False).wait_send()
        for p in range(len(pieces)):
            for copy in corner_copies(p) + mate_copies(p):
                copy.wait_send()

    each_plane(lambda zv: [sent])
    w_copy(0, 0, mate).wait_send()

    @pl.when(has_after)
    def _():
        w_copy(0, 1, after).wait_send()

    @pl.when(has_before)
    def _():
        w_copy(4, 2, before).wait_send()

    @pl.when(jnp.where(core == 1, has_before, has_after))
    def _():
        w_forward(0).wait_send()

    x_save.wait()


def gather_front(block, block_input, seg_query, seg_keys, plan):
    where = plan[0]
    count = lax.axis_size("fsdp")
    depth = count // 8
    rows, window = block_input.shape[0], seg_keys.shape[1]
    early, late = transfer_pieces(plan, depth)
    shape = lambda n, d=D, t=BF: jax.ShapeDtypeStruct((n, d), t)
    dma = pltpu.SemaphoreType.DMA
    units = D // ROWS
    many = len(early) + len(late)
    chunks = many + 3 * sum(1 for piece in early if piece[0] == 0)
    got = jax.ShapeDtypeStruct((5, rows, D), BF)
    return pl.pallas_call(
        functools.partial(gather_front_kernel, depth, where, early, late),
        out_shape=(
            jax.ShapeDtypeStruct((count, *block.shape), BF), shape(window), got,
            shape(rows), shape(window), shape(window), shape(rows), shape(rows, LANES, F32),
        ),
        in_specs=[ANY, ANY, VM, VM],
        out_specs=[ANY] * 3 + [VM] * 5,
        scratch_shapes=[
            dma((chunks, 2)), dma((chunks,)), dma((chunks,)), dma((chunks,)), dma((chunks,)), dma((chunks,)),
            dma((many, 2)), dma((many, 2)), dma((5, chunks)), dma((5, chunks)), dma((4,)), dma((5,)),
            dma, pltpu.VMEM(block.shape, BF), pltpu.VMEM((window, D), BF), pltpu.VMEM((window, D), BF),
            pltpu.VMEM((3, units, DC, ROWS, LANES), BF), pltpu.VMEM((2, ROWS, LANES), BF), pltpu.VMEM((2, ROWS, LANES), BF),
            pltpu.VMEM((rows, window), F32), pltpu.VMEM((rows, window), F32), pltpu.VMEM((rows, window), BF), dma((3,)), dma,
        ],
        compiler_params=pltpu.CompilerParams(collective_id=0, has_side_effects=True, vmem_limit_bytes=VMEM_LIMIT),
        name="gather_front",
    )(block, block_input, seg_query, seg_keys)


def passed_along(value, steps):
    count = lax.axis_size("fsdp")
    first, last = (max(0, -steps), min(count, count - steps))
    return lax.ppermute(value, "fsdp", [(source, source + steps) for source in range(first, last)])


def window_of(rows):
    near = [rows if k == 0 else passed_along(rows, -k) for k in range(-REACH, REACH + 1)]
    return jnp.concatenate(near, axis=0)


def shards(kernels, block_input, params, cotangent, segment_ids):
    count = lax.axis_size("fsdp")
    me = lax.axis_index("fsdp")
    rows = block_input.shape[0]
    margin = REACH * rows
    seg_pad = jnp.pad(segment_ids, (margin, margin), constant_values=-1)
    seg_query = lax.dynamic_slice_in_dim(segment_ids, me * rows, rows, 0)
    seg_keys = lax.dynamic_slice_in_dim(seg_pad, me * rows, 2 * margin + rows, 0)
    plan = wire_plan(count, params.shape[1])
    where = plan[0]
    block = to_tiles(params, plan)
    if kernels:
        gathered, x_win, _, queries, key_win, value_win, attended, logs = gather_front(
            block, block_input, seg_query[:, None], seg_keys[None, :], plan
        )
    else:
        x_win = window_of(block_input)
        gathered = lax.all_gather(block, "fsdp", axis=0, tiled=False)
        queries, key_win, value_win, attended, logs = front(
            x_win, seg_query[:, None], seg_keys[None, :], gathered, where, rows
        )
    activations, mid_grad, att_grad, parts = middle(block_input, cotangent, attended, gathered, where)
    near, own, parts = back(
        x_win, seg_query[None, :], seg_keys[:, None], gathered, queries, key_win, value_win, att_grad, logs, parts, where
    )
    input_grad = mid_grad + own
    for k in range(-REACH, REACH + 1):
        if k != 0:
            part = near[(k + REACH) * rows : (k + REACH + 1) * rows]
            input_grad = input_grad + passed_along(part, k).astype(jnp.float32)
    summed = scatter_blocks(parts, kernels)
    param_grads = to_flat(summed, plan, params.shape[1])
    return (activations, input_grad.astype(jnp.bfloat16), param_grads)


def two_by_two(mesh):
    spans = np.array([device.coords for device in mesh.devices.flat])
    return tuple(spans.max(axis=0) - spans.min(axis=0))[:2] == (1, 1)


def solution(mesh):
    return jax.shard_map(
        functools.partial(shards, two_by_two(mesh)),
        mesh=mesh,
        in_specs=(P("fsdp", None), P(None, "fsdp"), P("fsdp", None), P()),
        out_specs=(P("fsdp", None), P("fsdp", None), P(None, "fsdp")),
        check_vma=False,
    )
```

time: 3010 us -> 621 us (0.21)
  the two profiles are of different devices: /device:TPU:0 before, /device:TPU:3 now
where the time goes in v1:
time: 621 us; the launch traced here: 613 us
  Pallas kernels  535 us (86%)
  waiting for transfers between devices  47.7 us (8%)
  starting transfers between devices  13.9 us (2%)
  local copies, waits for them, and re-layouts  11.6 us (2%)
    pallas_call x1, Pallas kernels, gather_front(): pl.pallas_call(functools.partial(gather_front_kernel, depth, where, early...  205 us
    pallas_call x1, Pallas kernels, scatter_blocks(): pl.pallas_call(functools.partial(scatter_kernel, depth), out_shape=jax.Sh...  139 us
    pallas_call x1, Pallas kernels, back(): pl.pallas_call(functools.partial(back_kernel, where), out_shape=(jax.Shap...  117 us
    pallas_call x1, Pallas kernels, middle(): pl.pallas_call(functools.partial(middle_kernel, where), out_shape=(shape(...  57.5 us
    ppermute x4, waiting for transfers between devices, passed_along(): lax.ppermute(value, 'fsdp', [(source, source + steps) for source in range...  47.7 us
  transfers between devices with their start and end apart: 6, of which 4 were waited for; matrix products, arithmetic and copies ran while one was open for 2% of the time, Pallas kernels for 0%

profile of v1, /device:TPU:3, one launch (start us, length us, event | category | flops | bytes accessed | tf_op | source)
XLA Modules:
  0.0 612.8 jit_solution(1281603359126144210)
XLA Ops:
  0.6 1.2 slice.18
  1.9 0.7 collective-permute-start
  2.6 0.8 pad_dynamic-slice_fusion
  3.4 0.8 dynamic_slice.16
  4.2 0.6 broadcast_in_dim.14.segq_ref
  4.7 0.8 broadcast_in_dim.16.segq_ref
  5.5 0.6 broadcast_in_dim.13.segk_ref
  6.1 1.3 broadcast_in_dim.17.segk_ref
  7.4 1.3 dynamic_slice.18
  8.7 1.2 dynamic-slice_bitcast_fusion.table_ref
  9.9 0.0 collective-permute-done.head_ref
  9.9 0.7 copy-done.2
  10.6 7.8 %to_tiles.1.block_ref = bf16[242,16,128]{2,1,0:T(8,128)(2,1)} custom-call(s32[81]{0:T(128)} %dynamic-slice_bitcast_fusion.table_ref, bf16[1,476288]{1,0:T(2,128)(2,1)} %line_ref.1, bf16[1,69632]{1,0:T(2,128)(2,1)} %copy-done.2), custom_call_target="tpu_custom_call" | custom-call | tf_op jit(solution)/shard_map/to_tiles/pallas_call | solution.py:239
  18.4 204.9 %gather_front.1 = (bf16[32,242,16,128]{3,2,1,0:T(8,128)(2,1)}, bf16[1920,1152]{1,0:T(8,128)(2,1)}, bf16[5,384,1152]{2,1,0:T(8,128)(2,1)}, bf16[384,1152]{1,0:T(8...) custom-call(bf16[242,16,128]{2,1,0:T(8,128)(2,1)} %to_tiles.1.block_, ...), custom_call_target="tpu_custom_call" | custom-call | tf_op jit(solution)/shard_map/gather_front/pallas_call | solution.py:1406
  223.4 57.5 %middle.1 = (bf16[384,1152]{1,0:T(8,128)(2,1)}, f32[384,1152]{1,0:T(8,128)}, bf16[384,1152]{1,0:T(8,128)(2,1)}, bf16[32,242,16,128]{3,2,1,0:T(8,128)(2,1)}) custom-call(bf16[384,1152]{1,0:T(8,128)(2,1)} %x_ref.1, bf16[384,1152]{1,0:T(8,128)(2,1)} %cot_ref.1, bf16[384,1152]{1,0:T(8,128)(2,1)} %get-tuple-element.19.attended_ref, ...), custom_call_target="tpu_custom_call" | custom-call | tf_op jit(solution)/shard_map/middle/pallas_call | solution.py:824
  280.8 116.8 %back.1 = (bf16[1920,1152]{1,0:T(8,128)(2,1)}, f32[384,1152]{1,0:T(8,128)}, bf16[32,242,16,128]{3,2,1,0:T(8,128)(2,1)}) custom-call(bf16[1920,1152]{1,0:T(8,128)(2,1)} %get-tuple-element.23.x_hbm_ref, s32[1,384]{1,0:T(1,128)} %broadcast_in_dim.14.segq_ref, s32[1920,1]{1,0:T(8,128)} %broadcast_in_dim.17.segk_ref, ...), custom_call_target="tpu_custom_call", output_to_operand_aliasing={{2}: (9, {})} | custom-call | tf_op jit(solution)/shard_map/back/pallas_call | solution.py:961
  397.6 139.2 %scatter_blocks.1.tile_ref = f32[242,16,128]{2,1,0:T(8,128)} custom-call(bf16[32,242,16,128]{3,2,1,0:T(8,128)(2,1)} %get-tuple-element.32.part_ref), custom_call_target="tpu_custom_call" | custom-call | tf_op jit(solution)/shard_map/scatter_blocks/pallas_call | solution.py:495
  536.8 8.4 %to_flat.1 = (f32[1,476288]{1,0:T(1,128)}, f32[1,69632]{1,0:T(1,128)}) custom-call(s32[81]{0:T(128)} %dynamic-slice_bitcast_fusion.table_ref, f32[242,16,128]{2,1,0:T(8,128)} %scatter_blocks.1.tile_ref), custom_call_target="tpu_custom_call" | custom-call | tf_op jit(solution)/shard_map/to_flat/pallas_call | solution.py:254
  545.2 2.6 collective-permute-start.5
  547.8 2.4 fusion.1
  550.2 2.2 collective-permute-start.1
  552.4 4.0 collective-permute-start.4
  556.4 1.9 collective-permute-start.3
  558.3 2.4 collective-permute-start.2
  560.7 0.0 collective-permute-done.5
  560.7 2.6 fusion
  563.4 11.0 %collective-permute-done.1 = bf16[384,1152]{1,0:T(8,128)(2,1)S(1)} collective-permute-done((bf16[384,1152]{1,0:T(8,128)(2,1)S(1)}, bf16[384,1152]{1,0:T(8,128)(2,1)S(1)}, u32[]{:S(2)}, u32[]{:S(2)}) %collective-permute-start.1) | collective-permute-done | bytes 884768 | tf_op jit(solution)/shard_map/ppermute | solution.py:1429
  574.4 27.2 %collective-permute-done.4 = bf16[384,1152]{1,0:T(8,128)(2,1)S(1)} collective-permute-done((bf16[384,1152]{1,0:T(8,128)(2,1)S(1)}, bf16[384,1152]{1,0:T(8,128)(2,1)S(1)}, u32[]{:S(2)}, u32[]{:S(2)}) %collective-permute-start.4) | collective-permute-done | bytes 884768 | tf_op jit(solution)/shard_map/ppermute | solution.py:1429
  601.6 7.0 %collective-permute-done.3 = bf16[384,1152]{1,0:T(8,128)(2,1)S(1)} collective-permute-done((bf16[384,1152]{1,0:T(8,128)(2,1)S(1)}, bf16[384,1152]{1,0:T(8,128)(2,1)S(1)}, u32[]{:S(2)}, u32[]{:S(2)}) %collective-permute-start.3) | collective-permute-done | bytes 884768 | tf_op jit(solution)/shard_map/ppermute | solution.py:1429
  608.6 2.5 collective-permute-done.2
  611.1 0.0 copy-done
  611.1 1.5 add_convert_fusion
  (4 shorter events, 0.0 us)
Async XLA Ops:
  1.9 8.0 %collective-permute-start = (bf16[1,69632]{1,0:T(2,128)(2,1)S(1)}, bf16[1,69632]{1,0:T(2,128)(2,1)S(1)}, u32[]{:S(2)}, u32[]{:S(2)}) collective-permute-start(bf16[1,69632]{1,0:T(2,128)(2,1)S(1)} %slice.18), channel_id=1, source_target_pairs={{0,31},{1,0},{2,1},{3,2},{4,3},{5,4},{6,5},{7,6},{8,7},{9,8},{10,9... | collective-permute-start | bytes 417800 | tf_op jit(solution)/shard_map/ppermute | solution.py:237
  9.9 0.7 copy-start.2
  545.2 15.6 %collective-permute-start.5 = (f32[1,69632]{1,0:T(1,128)}, f32[1,69632]{1,0:T(1,128)S(1)}, u32[]{:S(2)}, u32[]{:S(2)}) collective-permute-start(f32[1,69632]{1,0:T(1,128)} %get-tuple-element.34), channel_id=1, source_target_pairs={{0,1},{1,2},{2,3},{3,4},{4,5},{5,6},{6,7},{7,8},{8,9},{9,10},{10,1... | collective-permute-start | bytes 835592 | tf_op jit(solution)/shard_map/ppermute | solution.py:263
  547.8 63.3 %copy-start = (f32[384,1152]{1,0:T(8,128)S(1)}, f32[384,1152]{1,0:T(8,128)}, u32[]{:S(2)}) copy-start(f32[384,1152]{1,0:T(8,128)} %get-tuple-element.22) | copy-start | bytes 5308420
  547.8 63.3 %copy-start.1 = (f32[384,1152]{1,0:T(8,128)S(1)}, f32[384,1152]{1,0:T(8,128)}, u32[]{:S(2)}) copy-start(f32[384,1152]{1,0:T(8,128)} %get-tuple-element.30) | copy-start | bytes 5308420
  550.2 24.2 %collective-permute-start.1 = (bf16[384,1152]{1,0:T(8,128)(2,1)S(1)}, bf16[384,1152]{1,0:T(8,128)(2,1)S(1)}, u32[]{:S(2)}, u32[]{:S(2)}) collective-permute-start(bf16[384,1152]{1,0:T(8,128)(2,1)S(1)} %get-tuple-element.35), channel_id=1, source_target_pairs={{2,0},{3,1},{4,2},{5,3},{6,4},{7,5},{8,6},{9,7},{10,8},{11,9},{12,... | collective-permute-start | bytes 2654216 | tf_op jit(solution)/shard_map/ppermute | solution.py:1429
  552.4 49.2 %collective-permute-start.4 = (bf16[384,1152]{1,0:T(8,128)(2,1)S(1)}, bf16[384,1152]{1,0:T(8,128)(2,1)S(1)}, u32[]{:S(2)}, u32[]{:S(2)}) collective-permute-start(bf16[384,1152]{1,0:T(8,128)(2,1)S(1)} %get-tuple-element.36), channel_id=1, source_target_pairs={{0,2},{1,3},{2,4},{3,5},{4,6},{5,7},{6,8},{7,9},{8,10},{9,11},{10,... | collective-permute-start | bytes 2654216 | tf_op jit(solution)/shard_map/ppermute | solution.py:1429
  556.4 52.2 %collective-permute-start.3 = (bf16[384,1152]{1,0:T(8,128)(2,1)S(1)}, bf16[384,1152]{1,0:T(8,128)(2,1)S(1)}, u32[]{:S(2)}, u32[]{:S(2)}) collective-permute-start(bf16[384,1152]{1,0:T(8,128)(2,1)S(1)} %get-tuple-element.37), channel_id=1, source_target_pairs={{0,1},{1,2},{2,3},{3,4},{4,5},{5,6},{6,7},{7,8},{8,9},{9,10},{10,1... | collective-permute-start | bytes 2654216 | tf_op jit(solution)/shard_map/ppermute | solution.py:1429
  558.3 52.8 %collective-permute-start.2 = (bf16[384,1152]{1,0:T(8,128)(2,1)S(1)}, bf16[384,1152]{1,0:T(8,128)(2,1)S(1)}, u32[]{:S(2)}, u32[]{:S(2)}) collective-permute-start(bf16[384,1152]{1,0:T(8,128)(2,1)S(1)} %get-tuple-element.38), channel_id=1, source_target_pairs={{1,0},{2,1},{3,2},{4,3},{5,4},{6,5},{7,6},{8,7},{9,8},{10,9},{11,1... | collective-permute-start | bytes 2654216 | tf_op jit(solution)/shard_map/ppermute | solution.py:1429

commit v2 on v1

--- a/solution.py
+++ b/solution.py
@@ -289,224 +289,6 @@
     pl.semaphore_wait(barrier, sum(present))
 
 
-def scatter_kernel(
-    depth, part_ref, out_ref, held, mates, halfs, fulls, lines, load_sem, mate_send, mate_recv, half_send, half_recv, full_send, full_recv, line_send, line_recv
-):
-    me = lax.axis_index("fsdp")
-    core, x, y, z = place(me)
-    mate, x_near, y_near = index_of(1 - core, x, y, z), index_of(core, 1 - x, y, z), index_of(core, x, 1 - y, z)
-    half = part_ref.shape[1] // 2
-    halves = (pl.ds(0, half), pl.ds(half, half))
-    greet(
-        [(mate, None), (x_near, None), (y_near, None), (me - 8, z > 0), (me + 8, z < depth - 1)]
-    )
-
-    def remote(source, target, send, recv, device):
-        return pltpu.make_async_remote_copy(
-            src_ref=source, dst_ref=target, send_sem=send, recv_sem=recv, device_id=(device,), device_id_type=MESH
-        )
-
-    def level_at(step):
-        low, high = jnp.minimum(z, depth - 1 - z), jnp.maximum(z, depth - 1 - z)
-        side_up = depth - 1 - z >= z
-        single = high - low
-        distance_single = high - step
-        pair = (step - single) // 2
-        distance_pair = low - pair
-        first_of_pair = lax.rem(step - single, 2) == 0
-        distance = jnp.where(step < single, distance_single, distance_pair)
-        up = jnp.where(step < single, side_up, first_of_pair)
-        return jnp.where(up, z + distance, z - distance)
-
-    order = [level_at(step) for step in range(depth)]
-    def owner(level, slot, which_core):
-        return index_of(which_core, 1 - x if slot in (1, 3) else x, 1 - y if slot in (2, 3) else y, level)
-
-    def to_mate(step, slot):
-        return remote(
-            part_ref.at[owner(order[step], slot, 1 - core)],
-            mates.at[step, slot],
-            mate_send.at[step, slot],
-            mate_recv.at[step, slot],
-            mate,
-        )
-
-    def load(step, slot):
-        return pltpu.make_async_copy(part_ref.at[owner(order[step], slot, core)], held.at[step, slot], load_sem.at[step, slot])
-
-    slots = (3, 1, 2, 0)
-    for step in range(depth):
-        for slot in slots:
-            to_mate(step, slot).start()
-            load(step, slot).start()
-
-    tiles = max(t for t in range(1, 17) if half % t == 0)
-
-    def add(target, sources, first, count):
-        @pl.loop(0, count // tiles)
-        def _(i):
-            at = pl.ds(first + i * tiles, tiles)
-            total = target[at].astype(jnp.float32)
-            for source, shift in sources:
-                total = total + source[pl.ds(first - shift + i * tiles, tiles)].astype(jnp.float32)
-            target[at] = total.astype(target.dtype)
-
-    def corner_out(step):
-        return (
-            remote(held.at[step, 3, halves[0]], halfs.at[step, 0], half_send.at[step, 0], half_recv.at[step, 0], y_near),
-            remote(held.at[step, 3, halves[1]], halfs.at[step, 1], half_send.at[step, 1], half_recv.at[step, 1], x_near),
-        )
-
-    def full_out(step):
-        return (
-            remote(held.at[step, 1], fulls.at[step, 0], full_send.at[step, 0], full_recv.at[step, 0], x_near),
-            remote(held.at[step, 2], fulls.at[step, 1], full_send.at[step, 1], full_recv.at[step, 1], y_near),
-        )
-
-    def line_out(step, up):
-        level = order[step]
-        if up:
-            return remote(held.at[step, 0], lines.at[level], line_send.at[step], line_recv.at[level], me + 8)
-        slot = jnp.where(level == z - 1, depth, level)
-        return remote(held.at[step, 0], lines.at[slot], line_send.at[step], line_recv.at[slot], me - 8)
-
-    def line_in(slot):
-        remote(held.at[0, 0], lines.at[slot], line_send.at[0], line_recv.at[slot], me).wait_recv()
-
-    def chip_sum(step, slot):
-        to_mate(step, slot).wait_recv()
-        load(step, slot).wait()
-        add(held.at[step, slot], [(mates.at[step, slot], 0)], 0, 2 * half)
-
-    def begin(step):
-        chip_sum(step, 3)
-        for c in corner_out(step):
-            c.start()
-        chip_sum(step, 1)
-        chip_sum(step, 2)
-        chip_sum(step, 0)
-
-    def middle(step):
-        by_y, by_x = corner_out(step)
-        by_y.wait_recv()
-        add(held.at[step, 1], [(halfs.at[step, 0], 0)], 0, half)
-        to_x, to_y = full_out(step)
-        to_x.start()
-        by_x.wait_recv()
-        add(held.at[step, 2], [(halfs.at[step, 1], half)], half, half)
-        to_y.start()
-
-    def end(step):
-        level = order[step]
-        to_x, to_y = full_out(step)
-        to_x.wait_recv()
-        to_y.wait_recv()
-        if step < depth - 1:
-            near = [(fulls.at[step, 0], 0), (fulls.at[step, 1], 0)]
-
-            @pl.when(level > z)
-            def _():
-                @pl.when(z > 0)
-                def _():
-                    line_in(level)
-                    add(held.at[step, 0], near + [(lines.at[level], 0)], 0, 2 * half)
-
-                @pl.when(z == 0)
-                def _():
-                    add(held.at[step, 0], near, 0, 2 * half)
-
-                line_out(step, True).start()
-
-            @pl.when(level < z)
-            def _():
-                @pl.when(z < depth - 1)
-                def _():
-                    line_in(level)
-                    add(held.at[step, 0], near + [(lines.at[level], 0)], 0, 2 * half)
-
-                @pl.when(z == depth - 1)
-                def _():
-                    add(held.at[step, 0], near, 0, 2 * half)
-
-                line_out(step, False).start()
-
-    def total():
-        step = depth - 1
-
-        def write(sources):
-            @pl.loop(0, 2 * half // tiles)
-            def _(i):
-                at = pl.ds(i * tiles, tiles)
-                value = held[step, 0, at].astype(jnp.float32)
-                for source in sources:
-                    value = value + source[at].astype(jnp.float32)
-                out_ref[at] = value
-
-        near = [fulls.at[step, 0], fulls.at[step, 1]]
-
-        @pl.when(z > 0)
-        def _():
-            line_in(z)
-
-        @pl.when(z < depth - 1)
-        def _():
-            line_in(depth)
-
-        @pl.when((z > 0) & (z < depth - 1))
-        def _():
-            write(near + [lines.at[z], lines.at[depth]])
-
-        @pl.when(z == 0)
-        def _():
-            write(near + [lines.at[depth]])
-
-        @pl.when(z == depth - 1)
-        def _():
-            write(near + [lines.at[z]])
-
-    for step in range(depth):
-        begin(step)
-        if step >= 1:
-            middle(step - 1)
-        if step >= 2:
-            end(step - 2)
-    middle(depth - 1)
-    end(depth - 2)
-    end(depth - 1)
-    total()
-    for step in range(depth):
-        for slot in slots:
-            to_mate(step, slot).wait_send()
-        for c in corner_out(step) + full_out(step):
-            c.wait_send()
-        if step < depth - 1:
-            line_out(step, True).wait_send()
-
-
-def scatter_blocks(parts, kernels):
-    count, block = parts.shape[:2]
-    if not kernels:
-        received = lax.all_to_all(parts, "fsdp", split_axis=0, concat_axis=0, tiled=True)
-        return jnp.sum(received.astype(jnp.float32), axis=0)
-    depth = count // 8
-    dma = pltpu.SemaphoreType.DMA
-    full, part = (block, ROWS, LANES), (block // 2, ROWS, LANES)
-    vmem = lambda lead, shape: pltpu.VMEM((*lead, *shape), parts.dtype)
-    return pl.pallas_call(
-        functools.partial(scatter_kernel, depth),
-        out_shape=jax.ShapeDtypeStruct(full, jnp.float32),
-        in_specs=[pl.BlockSpec(memory_space=pl.ANY)],
-        out_specs=pl.BlockSpec(memory_space=pltpu.VMEM),
-        scratch_shapes=[
-            vmem((depth, 4), full), vmem((depth, 4), full), vmem((depth, 2), part), vmem((depth, 2), full), vmem((depth + 1,), full),
-            dma((depth, 4)), dma((depth, 4)), dma((depth, 4)), dma((depth, 2)), dma((depth, 2)), dma((depth, 2)), dma((depth, 2)),
-            dma((depth,)), dma((depth + 1,)),
-        ],
-        compiler_params=pltpu.CompilerParams(collective_id=1, has_side_effects=True, vmem_limit_bytes=62 << 20),
-        name="scatter_blocks",
-    )(parts)
-
-
 BF = jnp.bfloat16
 F32 = jnp.float32
 PAIR = 2 * LANES
@@ -619,7 +401,7 @@
 
 
 def front_kernel(
-    where, x_ref, segq_ref, segk_ref, blocks_ref, q_ref, k_ref, v_ref, attended_ref, logs_ref,
+    where, x_ref, segq_ref, segk_ref, blocks_ref, q_ref, k_ref, v_ref, attended_ref, rest_ref, logs_ref,
     normed_ref, w_ref, vec1_ref, vec2_ref, bias_ref, score_ref, prob_ref, sem, vec_sem,
 ):
     window, rows = x_ref.shape[0], q_ref.shape[0]
@@ -664,6 +446,7 @@
                     out[at, lanes] = (nn(normed_ref[at], weights) + add[:, lanes]).astype(BF)
 
     attended_ref[...] = jnp.zeros_like(attended_ref)
+    rest_ref[...] = jnp.zeros_like(rest_ref)
     logs_ref[...] = jnp.zeros_like(logs_ref)
     lane_l = lax.broadcasted_iota(jnp.int32, logs_ref.shape, 1)
 
@@ -679,7 +462,9 @@
         total = jnp.sum(powers, axis=-1, keepdims=True)
         prob_ref[...] = powers.astype(BF)
         out = nn(prob_ref[...], v_ref[:, lanes]) / total
-        attended_ref[:, lanes] = jnp.where(mask, out.astype(BF), attended_ref[:, lanes])
+        rounded = out.astype(BF)
+        attended_ref[:, lanes] = jnp.where(mask, rounded, attended_ref[:, lanes])
+        rest_ref[:, lanes] = jnp.where(mask, (out - rounded.astype(F32)).astype(BF), rest_ref[:, lanes])
         logs_ref[...] = jnp.where(lane_l == h, top + jnp.log(total), logs_ref[...])
 
 
@@ -690,9 +475,9 @@
     units = D // ROWS
     return pl.pallas_call(
         functools.partial(front_kernel, where),
-        out_shape=(shape(rows), shape(window), shape(window), shape(rows), shape(rows, LANES, F32)),
+        out_shape=(shape(rows), shape(window), shape(window), shape(rows), shape(rows), shape(rows, LANES, F32)),
         in_specs=[VM, VM, VM, ANY],
-        out_specs=[VM] * 5,
+        out_specs=[VM] * 6,
         scratch_shapes=[
             pltpu.VMEM((window, D), BF),
             pltpu.VMEM((3, units, DC, ROWS, LANES), BF), pltpu.VMEM((2, ROWS, LANES), BF), pltpu.VMEM((2, ROWS, LANES), BF),
@@ -704,7 +489,7 @@
 
 
 def middle_kernel(
-    where, x_ref, cot_ref, attended_ref, blocks_ref, act_ref, mid_grad_ref, att_grad_ref, parts_ref,
+    where, x_ref, cot_ref, attended_ref, rest_ref, blocks_ref, act_ref, mid_grad_ref, att_grad_ref, delta_ref, parts_ref,
     wo_ref, wu_ref, wd_ref, vec3_ref, vec4_ref, vec5_ref, b_up_ref, hidden_ref, slope_ref, pre_ref, normed_ref, normed_b_ref,
     mid_ref, g_up_ref, sem, out_sem,
 ):
@@ -798,6 +583,8 @@
         lanes = slice(c * LANES, (c + many) * LANES)
         weights = panels(wo_ref, 0, DC, many * LANES // ROWS, c * LANES // ROWS)
         att_grad_ref[:, lanes] = nt(mid_b, weights).astype(BF)
+    product = att_grad_ref[...].astype(F32) * (attended_ref[...].astype(F32) + rest_ref[...].astype(F32))
+    delta_ref[...] = jnp.sum(product.T.reshape(HEADS, HEAD_DIM, rows), axis=1)
     turned = attended_ref[...].T
     for c in range(0, DC, 2):
         many = min(2, DC - c)
@@ -815,7 +602,7 @@
         wait(saves[n])
 
 
-def middle(block_input, cotangent, attended, gathered, where):
+def middle(block_input, cotangent, attended, rest, gathered, where):
     rows = block_input.shape[0]
     shape = lambda t: jax.ShapeDtypeStruct((rows, D), t)
     dma = pltpu.SemaphoreType.DMA
@@ -823,9 +610,9 @@
     units, f_wide = D // ROWS, FC * LANES
     return pl.pallas_call(
         functools.partial(middle_kernel, where),
-        out_shape=(shape(BF), shape(F32), shape(BF), jax.ShapeDtypeStruct(gathered.shape, BF)),
-        in_specs=[VM, VM, VM, ANY],
-        out_specs=[VM, VM, VM, ANY],
+        out_shape=(shape(BF), shape(F32), shape(BF), jax.ShapeDtypeStruct((HEADS, rows), F32), jax.ShapeDtypeStruct(gathered.shape, BF)),
+        in_specs=[VM, VM, VM, VM, ANY],
+        out_specs=[VM, VM, VM, VM, ANY],
         scratch_shapes=[
             tiles(units, DC), tiles(units, FC), tiles(f_wide // ROWS, DC), tiles(2), tiles(3), tiles(DC),
             pltpu.VMEM((3 * ROWS, LANES), F32), pltpu.VMEM((rows, f_wide), BF), pltpu.VMEM((rows, f_wide), F32),
@@ -834,7 +621,7 @@
         ],
         compiler_params=pltpu.CompilerParams(vmem_limit_bytes=VMEM_LIMIT),
         name="middle",
-    )(block_input, cotangent, attended, gathered)
+    )(block_input, cotangent, attended, rest, gathered)
 
 
 def back_kernel(
@@ -980,22 +767,22 @@
 
 
 def transfer_pieces(plan, depth):
-    where, block = plan[:2]
+    where = plan[0]
     count = plan[2].shape[0]
-    hot = [0] * depth
-    for name in HOT_NAMES:
+    hot, used = [0] * depth, [0] * depth
+    for name in where:
         for owner, at, tiles in where[name]:
             level = owner * depth // count
-            hot[level] = max(hot[level], at + tiles)
-    hot = [min(block, h + h % 2) for h in hot]
+            used[level] = max(used[level], at + tiles)
+            if name in HOT_NAMES:
+                hot[level] = max(hot[level], at + tiles)
     early = [(level, 0, h) for level, h in enumerate(hot) if h]
-    late = [(level, h, block - h) for level, h in enumerate(hot) if h < block]
+    late = [(level, h, u - h) for level, (h, u) in enumerate(zip(hot, used)) if h < u]
     return early, late
 
 
 def cut(piece, many):
     level, first, tiles = piece
-    edges = [tiles // 2 * i // (many // 2) if i <= many // 2 else 0 for i in range(many // 2 + 1)]
     half = tiles // 2
     edges = [half * i // (many // 2) for i in range(many // 2)] + [
         half + (tiles - half) * i // (many // 2) for i in range(many // 2 + 1)
@@ -1006,7 +793,7 @@
 def gather_front_kernel(
     depth, where, early, late,
     block_ref, x_in_ref, segq_ref, segk_ref,
-    out_ref, x_out_ref, x_got_ref, q_ref, k_ref, v_ref, attended_ref, logs_ref,
+    out_ref, x_out_ref, x_got_ref, q_ref, k_ref, v_ref, attended_ref, rest_ref, logs_ref,
     z_send, z_recv, x_send, x_recv, y_send, y_recv, corner_send, corner_recv, mate_send, mate_recv, w_send, w_recv,
     local_sem, stage_ref, x_ref, normed_ref, w_ref, vec1_ref, vec2_ref, bias_ref, score_ref, prob_ref, sem, vec_sem,
 ):
@@ -1328,6 +1115,7 @@
         if i == 1:
             service("takes")
     attended_ref[...] = jnp.zeros_like(attended_ref)
+    rest_ref[...] = jnp.zeros_like(rest_ref)
     logs_ref[...] = jnp.zeros_like(logs_ref)
     lane_l = lax.broadcasted_iota(jnp.int32, logs_ref.shape, 1)
     when = {("beside", k): (0, 4, 10)[min(k, 2)] for k in range(len(cold))}
@@ -1352,7 +1140,9 @@
         total = jnp.sum(powers, axis=-1, keepdims=True)
         prob_ref[...] = powers.astype(BF)
         out = nn(prob_ref[...], v_ref[:, lanes]) / total
-        attended_ref[:, lanes] = jnp.where(mask, out.astype(BF), attended_ref[:, lanes])
+        rounded = out.astype(BF)
+        attended_ref[:, lanes] = jnp.where(mask, rounded, attended_ref[:, lanes])
+        rest_ref[:, lanes] = jnp.where(mask, (out - rounded.astype(F32)).astype(BF), rest_ref[:, lanes])
         logs_ref[...] = jnp.where(lane_l == h, top + jnp.log(total), logs_ref[...])
 
     for name, at_head in when.items():
@@ -1407,10 +1197,10 @@
         functools.partial(gather_front_kernel, depth, where, early, late),
         out_shape=(
             jax.ShapeDtypeStruct((count, *block.shape), BF), shape(window), got,
-            shape(rows), shape(window), shape(window), shape(rows), shape(rows, LANES, F32),
+            shape(rows), shape(window), shape(window), shape(rows), shape(rows), shape(rows, LANES, F32),
         ),
         in_specs=[ANY, ANY, VM, VM],
-        out_specs=[ANY] * 3 + [VM] * 5,
+        out_specs=[ANY] * 3 + [VM] * 6,
         scratch_shapes=[
             dma((chunks, 2)), dma((chunks,)), dma((chunks,)), dma((chunks,)), dma((chunks,)), dma((chunks,)),
             dma((many, 2)), dma((many, 2)), dma((5, chunks)), dma((5, chunks)), dma((4,)), dma((5,)),
@@ -1421,6 +1211,517 @@
         compiler_params=pltpu.CompilerParams(collective_id=0, has_side_effects=True, vmem_limit_bytes=VMEM_LIMIT),
         name="gather_front",
     )(block, block_input, seg_query, seg_keys)
+
+
+def back_scatter_kernel(
+    depth, where, early, late,
+    x_hbm_ref, segq_ref, segk_ref, blocks_ref, q_ref, k_hbm_ref, v_hbm_ref, grad_ref, logs_ref, delta_ref, mid_hbm_ref, parts_in_ref,
+    parts_ref, out_ref, in_grad_ref, mates, sums, halfs, fulls, lines, near_ref, near_got,
+    w_ref, g_ref, vec1_ref, vec2_ref, score_ref, prob_ref, turned_ref, k_ref, v_ref, dq_ref, part_ref, logs_t_ref, x_ref,
+    block_ref, mid_ref, g_value_ref, gain_acc, shift_acc, stage, total,
+    mate_send, mate_recv, half_send, half_recv, full_send, full_recv, line_send, line_recv, near_send, near_recv,
+    load_sem, store_sem, sem, vec_sem, out_sem, x_sem,
+):
+    me = lax.axis_index("fsdp")
+    count = 8 * depth
+    core, x, y, z = place(me)
+    mate, x_near, y_near = index_of(1 - core, x, y, z), index_of(core, 1 - x, y, z), index_of(core, x, 1 - y, z)
+    after, before = me + 2, me - 2
+    has_after, has_before = after < count, before >= 0
+    greet(
+        [(mate, None), (x_near, None), (y_near, None), (me - 8, z > 0), (me + 8, z < depth - 1), (after, has_after), (before, has_before)]
+    )
+    pieces = early + late
+    early_ids, late_ids = range(len(early)), range(len(early), len(pieces))
+
+    def remote(source, target, send, recv, device):
+        return pltpu.make_async_remote_copy(
+            src_ref=source, dst_ref=target, send_sem=send, recv_sem=recv, device_id=(device,), device_id_type=MESH
+        )
+
+    def owner(level, slot, which_core):
+        return index_of(which_core, 1 - x if slot in (1, 3) else x, 1 - y if slot in (2, 3) else y, level)
+
+    def at_plane(zv, run):
+        @pl.when(z == zv)
+        def _():
+            run()
+
+    def span(p, lo=0, many=None):
+        _, first, tiles = pieces[p]
+        return pl.ds(first + lo, tiles if many is None else many)
+
+    def half_of(p):
+        return pieces[p][2] // 2
+
+    def to_mate(p, slot):
+        level = pieces[p][0]
+        return remote(
+            parts_ref.at[owner(level, slot, 1 - core), span(p)], mates.at[level, slot, span(p)],
+            mate_send.at[p, slot], mate_recv.at[p, slot], mate,
+        )
+
+    def half_out(p, side):
+        level, _, tiles = pieces[p]
+        part = span(p, half_of(p), tiles - half_of(p)) if side else span(p, 0, half_of(p))
+        return remote(
+            sums.at[level, 3, part], halfs.at[level, side, part], half_send.at[p, side], half_recv.at[p, side],
+            x_near if side else y_near,
+        )
+
+    def full_out(p, side):
+        level = pieces[p][0]
+        return remote(
+            sums.at[level, 1 + side, span(p)], fulls.at[level, side, span(p)], full_send.at[p, side], full_recv.at[p, side],
+            y_near if side else x_near,
+        )
+
+    def line_out(p, zv):
+        level = pieces[p][0]
+        upward = level > zv
+        slot = depth if not upward and level == zv - 1 else level
+        side = 1 if slot == depth else 0
+        return remote(
+            sums.at[level, 0, span(p)], lines.at[slot, span(p)], line_send.at[p], line_recv.at[p, side],
+            me + 8 if upward else me - 8,
+        )
+
+    def line_in(p, side):
+        level = pieces[p][0]
+        slot = depth if side else level
+        return remote(sums.at[level, 0, span(p)], lines.at[slot, span(p)], line_send.at[p], line_recv.at[p, side], me)
+
+    def line_sides(p, zv):
+        level = pieces[p][0]
+        if level > zv:
+            return [0] if zv > 0 else []
+        if level < zv:
+            return [0] if zv < depth - 1 else []
+        return ([0] if zv > 0 else []) + ([1] if zv < depth - 1 else [])
+
+    def sources(kind, p, zv):
+        level, _, tiles = pieces[p]
+        h = half_of(p)
+        found = [(parts_ref.at[owner(level, kind, core), span(p)], 0, tiles), (mates.at[level, kind, span(p)], 0, tiles)]
+        if kind == 1:
+            found.append((halfs.at[level, 0, span(p, 0, h)], 0, h))
+        if kind == 2:
+            found.append((halfs.at[level, 1, span(p, h, tiles - h)], h, tiles - h))
+        if kind == 0:
+            found += [(fulls.at[level, side, span(p)], 0, tiles) for side in (0, 1)]
+            found += [(lines.at[depth if side else level, span(p)], 0, tiles) for side in line_sides(p, zv)]
+        return found
+
+    def loads(kind, p, zv, base):
+        return [
+            pltpu.make_async_copy(ref, stage.at[i, pl.ds(base + lo, many)], load_sem.at[1 if base else 0])
+            for i, (ref, lo, many) in enumerate(sources(kind, p, zv))
+        ]
+
+    def store(kind, p, base):
+        level, _, tiles = pieces[p]
+        return pltpu.make_async_copy(
+            total.at[pl.ds(base, tiles)], sums.at[level, kind, span(p)], store_sem.at[1 if base else 0]
+        )
+
+    def load(kind, p, zv, base=0):
+        to_mate(p, kind).wait_recv()
+        if kind in (1, 2):
+            half_out(p, kind - 1).wait_recv()
+        if kind == 0:
+            for side in (0, 1):
+                full_out(p, side).wait_recv()
+            for side in line_sides(p, zv):
+                line_in(p, side).wait_recv()
+        start(loads(kind, p, zv, base))
+
+    def add(base, lo, many, slots, target, shift):
+        def some(first, tiles):
+            value = stage[slots[0], pl.ds(first, tiles)].astype(F32)
+            for slot in slots[1:]:
+                value = value + stage[slot, pl.ds(first, tiles)].astype(F32)
+            target[pl.ds(first + shift, tiles)] = value.astype(target.dtype)
+
+        group = 8
+
+        @pl.loop(0, many // group)
+        def _(i):
+            some(base + lo + i * group, group)
+
+        if many % group:
+            some(base + lo + many // group * group, many % group)
+
+    def finish(kind, p, zv, base=0):
+        level, first, tiles = pieces[p]
+        found = sources(kind, p, zv)
+        wait(loads(kind, p, zv, base))
+        final = kind == 0 and level == zv
+        target, shift = (out_ref, first - base) if final else (total, 0)
+        edges = sorted({e for _, lo, many in found for e in (lo, lo + many)})
+        for lo, hi in zip(edges[:-1], edges[1:]):
+            slots = [i for i, (_, a, many) in enumerate(found) if a <= lo and hi <= a + many]
+            add(base, lo, hi - lo, slots, target, shift)
+        if not final:
+            store(kind, p, base).start()
+
+    def send(kind, p, zv, base=0):
+        if kind == 0 and pieces[p][0] == zv:
+            return
+        store(kind, p, base).wait()
+        if kind == 3:
+            half_out(p, 0).start()
+            half_out(p, 1).start()
+        elif kind == 0:
+            line_out(p, zv).start()
+        else:
+            full_out(p, kind - 1).start()
+
+    def run(jobs, zv, ahead=False):
+        bases = [(k % 2) * (stage.shape[1] // 2) if ahead else 0 for k in range(len(jobs))]
+        for k, (kind, p) in enumerate(jobs):
+            if k == 0 or not ahead:
+                load(kind, p, zv, bases[k])
+            if ahead and k + 1 < len(jobs):
+                load(*jobs[k + 1], zv, bases[k + 1])
+            finish(kind, p, zv, bases[k])
+            send(kind, p, zv, bases[k])
+
+    for p in early_ids:
+        for slot in (3, 1, 2, 0):
+            to_mate(p, slot).start()
+
+    window, rows = k_ref.shape[0], q_ref.shape[0]
+    margin = (window - rows) // 2
+    names = ("w_query", "w_key", "w_value")
+    k_load = [pltpu.make_async_copy(k_hbm_ref, k_ref, vec_sem), pltpu.make_async_copy(v_hbm_ref, v_ref, vec_sem)]
+    start(k_load)
+    weight_loads = [copies(where, name, blocks_ref, w_ref.at[i], sem.at[i]) for i, name in enumerate(names)]
+    vecs = copies(where, "vec1", blocks_ref, vec1_ref, sem.at[3])
+    start(vecs)
+    for made in weight_loads:
+        start(made)
+    x_load = [pltpu.make_async_copy(x_hbm_ref, x_ref, x_sem)]
+    start(x_load)
+    wait(k_load)
+
+    @pl.loop(0, window // LANES)
+    def _(i):
+        at = pl.ds(pl.multiple_of(i * LANES, LANES), LANES)
+        turned_ref[:, at] = k_ref[at].T
+
+    logs_t_ref[...] = logs_ref[...].T
+    g_value_ref[...] = jnp.zeros_like(g_value_ref)
+
+    by_level = {pieces[p][0]: p for p in early_ids}
+    a, b, c_ = (by_level[level] for level in sorted(by_level, reverse=True)[:3])
+    table = [
+        (-1, 0, 3, a, None), (0, 1, 3, b, None), (3, 4, 1, a, None), (4, 5, 2, a, None), (5, 6, 3, c_, None),
+        (6, 7, 1, b, None), (7, 8, 2, b, None), (11, 12, 0, a, 0), (12, 13, 1, c_, None), (13, 14, 2, c_, None),
+    ]
+
+    def beside(h, which, action):
+        for entry in table:
+            if entry[which] < 0:
+                continue
+            kind, p, zv = entry[2:]
+            there = h == entry[which]
+            if zv is not None:
+                there = there & (z == zv)
+
+            @pl.when(there)
+            def _():
+                action(kind, p, zv)
+
+    load(3, a, None)
+
+    @pl.loop(0, HEADS)
+    def _(h):
+        beside(h, 1, finish)
+        lane, offset = head_window(h)
+        mask = head_mask(rows, offset)
+        lanes = pl.ds(lane, PAIR)
+        query = jnp.where(mask, q_ref[:, lanes], jnp.zeros((), BF))
+        grad = jnp.where(mask, grad_ref[:, lanes], jnp.zeros((), BF))
+        log_row, delta_row = logs_t_ref[pl.ds(h, 1)], delta_ref[pl.ds(h, 1)]
+        blocks = [pl.ds(n * rows, rows) for n in range(window // rows)]
+        for keys in blocks:
+            together = jnp.concatenate([segk_ref[keys]] * (rows // LANES), axis=1) == segq_ref[...]
+            probs = jnp.exp(jnp.where(together, nt(k_ref[keys, lanes], query) * SCALE - log_row, NEG))
+            prob_ref[keys] = probs.astype(BF)
+            score_ref[keys] = (probs * (nt(v_ref[keys, lanes], grad) - delta_row)).astype(BF)
+        beside(h, 1, send)
+        beside(h, 0, load)
+        side = head_mask(rows, offset)
+        for keys in blocks:
+            dv = nn(prob_ref[keys], grad)
+            g_value_ref[:, lanes] += column_sums(dv)
+            v_ref[keys, lanes] = jnp.where(side, dv.astype(BF), v_ref[keys, lanes])
+            dk = nn(score_ref[keys], query) * SCALE
+            k_ref[keys, lanes] = jnp.where(side, dk.astype(BF), k_ref[keys, lanes])
+        part_ref[...] = nn(turned_ref[lanes], score_ref[...])
+        at = pl.ds(pl.multiple_of(h * HEAD_DIM, 8), HEAD_DIM)
+        dq_ref[at] = part_ref[pl.ds(pl.multiple_of(offset, 8), HEAD_DIM)]
+
+    dq = dq_ref[...].T * SCALE
+    put_vectors(vec2_ref, [column_sums(dq), g_value_ref[...]])
+    saves = copies(where, "vec2", parts_ref, vec2_ref, out_sem.at[3], out=True)
+    dq_b = dq.astype(BF)
+    wait(vecs)
+    vec = vector_rows(vec1_ref)
+    gain, shift = as_row(vec, 0, DC), as_row(vec, DC, DC)
+    gain_t, shift_t = (jnp.broadcast_to(v, (8, D)).T[:, :1] for v in (gain, shift))
+    wait(x_load)
+    step = rows // 3
+
+    @pl.loop(0, window // step)
+    def _(i):
+        at = pl.ds(pl.multiple_of(i * step, step), step)
+        normed, _ = norm_rows(x_ref[at].astype(F32))
+        turned_ref[:, at] = normed.astype(BF).T
+
+    for made in weight_loads:
+        wait(made)
+    gain_acc[...] = jnp.zeros_like(gain_acc)
+    shift_acc[...] = jnp.zeros_like(shift_acc)
+
+    later = {
+        (1, 0): [("load", [(1, a), (0, b), (3, b)])], (1, 1): [("end", [(1, a), (0, b), (3, b)])],
+        (2, 0): [("load", [(0, c_), (3, c_)])],
+    }
+
+    def plane_job(what, entries):
+        for zv, p in entries:
+
+            def go():
+                if what == "load":
+                    load(0, p, zv)
+                else:
+                    finish(0, p, zv)
+                    send(0, p, zv)
+
+            at_plane(zv, go)
+
+    own = turned_ref[:, pl.ds(margin, rows)]
+    made = []
+    for i, (left, right_ref) in enumerate(((own, None), (turned_ref, k_ref), (turned_ref, v_ref))):
+        if i == 2:
+            wait(made[0])
+        for pair, c in enumerate(range(0, DC, 2)):
+            for what, entries in later.get((i, pair), []):
+                plane_job(what, entries)
+            many = min(2, DC - c)
+            lanes = slice(c * LANES, (c + many) * LANES)
+            right = dq_b[:, lanes] if right_ref is None else right_ref[:, lanes]
+            raw = nn(left[...], right)
+            summed = column_sums(right.astype(F32))
+            put_panels(g_ref.at[i % 2], c, gain_t * raw + shift_t * summed)
+            weights = panels(w_ref.at[i], c, many, D // ROWS).astype(F32)
+            scaled, shifted = weights * raw, weights * summed
+            for j in range(many):
+                part = slice(j * LANES, (j + 1) * LANES)
+                gain_acc[...] += scaled[:, part]
+                shift_acc[...] += shifted[:, part]
+        made.append(copies(where, names[i], parts_ref, g_ref.at[i % 2], out_sem.at[i], out=True))
+        start(made[i])
+    put_vectors(vec1_ref, [column_sums(gain_acc[...].T), column_sums(shift_acc[...].T)])
+    saves = saves + copies(where, "vec1", parts_ref, vec1_ref, out_sem.at[3], out=True)
+    start(saves)
+    plane_job("end", [(0, c_), (3, c_)])
+    wait(saves + made[1] + made[2])
+    for p in late_ids:
+        for slot in (3, 1, 2, 0):
+            to_mate(p, slot).start()
+
+    def row_block(n):
+        first = n * rows
+        own = n == window // rows // 2
+        for c in range(0, DC, 2):
+            many = min(2, DC - c)
+            lanes = slice(c * LANES, (c + many) * LANES)
+            part = lambda i: panels(w_ref.at[i], 0, DC, many * LANES // ROWS, c * LANES // ROWS)
+            value = nt(k_ref[first : first + rows], part(1)) + nt(v_ref[first : first + rows], part(2))
+            if own:
+                value = value + nt(dq_b, part(0))
+            block_ref[:, lanes] = value
+
+        @pl.loop(0, rows // step)
+        def _(i):
+            here = pl.ds(pl.multiple_of(i * step, step), step)
+            there = pl.ds(pl.multiple_of(first + i * step, step), step)
+            normed, inverse = norm_rows(x_ref[there].astype(F32))
+            result = norm_rows_back(block_ref[here], normed, inverse, gain)
+            if own:
+                block_ref[here] = result
+            else:
+                x_ref[there] = result.astype(BF)
+
+    def near_rows(slot):
+        return x_ref.at[pl.ds(slot * rows, rows)]
+
+    def near_save(slot):
+        return pltpu.make_async_copy(near_rows(slot), near_ref.at[slot], x_sem)
+
+    def near_copy(slot, which, device):
+        return remote(near_ref.at[slot], near_got.at[which], near_send.at[which], near_recv.at[which], device)
+
+    row_block(0)
+    row_block(4)
+    ends = [near_save(0), near_save(4)]
+    start(ends)
+    at_plane(1, lambda: run([(0, b)], 1))
+    at_plane(2, lambda: run([(0, a), (0, c_)], 2))
+    run([(3, p) for p in late_ids], None, True)
+    row_block(1)
+    row_block(3)
+    wait(ends)
+    sides = [near_save(1), near_save(3)]
+    start(sides)
+    wait(sides)
+    to_mate_itself, to_mate_shared = (3 - 2 * core), (1 + 2 * core)
+    near_copy(to_mate_itself, 0, mate).start()
+    near_copy(to_mate_shared, 1, mate).start()
+
+    @pl.when((core == 0) & has_before)
+    def _():
+        near_copy(0, 2, before).start()
+
+    @pl.when((core == 1) & has_after)
+    def _():
+        near_copy(4, 3, after).start()
+
+    run([(kind, p) for p in late_ids for kind in (1, 2)], None)
+    row_block(2)
+    near_copy(0, 1, me).wait_recv()
+    shared_slot = 4 - 4 * core
+    fetch = pltpu.make_async_copy(near_got.at[1], k_ref.at[pl.ds(0, rows)], x_sem)
+    fetch.start()
+    fetch.wait()
+
+    @pl.loop(0, rows // step)
+    def _(i):
+        here = pl.ds(pl.multiple_of(i * step, step), step)
+        there = pl.ds(pl.multiple_of(shared_slot * rows + i * step, step), step)
+        x_ref[there] = (x_ref[there].astype(F32) + k_ref[here].astype(F32)).astype(BF)
+
+    shared_save = near_save(shared_slot)
+    shared_save.start()
+    shared_save.wait()
+
+    @pl.when((core == 0) & has_after)
+    def _():
+        near_copy(4, 3, after).start()
+
+    @pl.when((core == 1) & has_before)
+    def _():
+        near_copy(0, 2, before).start()
+
+    def tail(zv):
+        out = [p for p in late_ids if pieces[p][0] != zv]
+        hops = lambda p: zv if pieces[p][0] > zv else depth - 1 - zv
+        moving = [(0, p) for p in sorted(out, key=lambda p: (hops(p), p))]
+        finals = [(0, p) for p in early_ids if pieces[p][0] == zv] + [(0, p) for p in late_ids if pieces[p][0] == zv]
+        return moving + finals
+
+    for zv in range(depth):
+        at_plane(zv, lambda: run(tail(zv), zv))
+
+    near_copy(0, 0, me).wait_recv()
+
+    @pl.when(has_after)
+    def _():
+        near_copy(0, 2, me).wait_recv()
+
+    @pl.when(has_before)
+    def _():
+        near_copy(0, 3, me).wait_recv()
+
+    for i, (which, there) in enumerate(((0, None), (2, has_after), (3, has_before))):
+        target = k_ref.at[pl.ds(i * rows, rows)]
+        if there is None:
+            pltpu.make_async_copy(near_got.at[which], target, x_sem).start()
+            continue
+
+        @pl.when(there)
+        def _():
+            pltpu.make_async_copy(near_got.at[which], target, x_sem).start()
+
+        @pl.when(jnp.logical_not(there))
+        def _():
+            pltpu.make_async_copy(near_ref.at[0], target, x_sem).start()
+
+    for i in range(3):
+        pltpu.make_async_copy(near_got.at[0], k_ref.at[pl.ds(i * rows, rows)], x_sem).wait()
+    near_after, near_before = (jnp.where(there, 1.0, 0.0) for there in (has_after, has_before))
+
+    @pl.loop(0, rows // step)
+    def _(i):
+        here = pl.ds(pl.multiple_of(i * step, step), step)
+        fetch_mid = pltpu.make_async_copy(mid_hbm_ref.at[here], mid_ref, x_sem)
+        fetch_mid.start()
+        fetch_mid.wait()
+        value = mid_ref[...] + block_ref[here] + k_ref[here].astype(F32)
+        value = value + near_after * k_ref[pl.ds(pl.multiple_of(rows + i * step, step), step)].astype(F32)
+        value = value + near_before * k_ref[pl.ds(pl.multiple_of(2 * rows + i * step, step), step)].astype(F32)
+        in_grad_ref[here] = value.astype(BF)
+
+    for p in range(len(pieces)):
+        for slot in range(4):
+            to_mate(p, slot).wait_send()
+        for side in (0, 1):
+            half_out(p, side).wait_send()
+            full_out(p, side).wait_send()
+        for zv in range(depth):
+            if pieces[p][0] != zv:
+                at_plane(zv, lambda: line_out(p, zv).wait_send())
+    near_copy(0, 0, mate).wait_send()
+    near_copy(0, 1, mate).wait_send()
+
+    @pl.when(has_before)
+    def _():
+        near_copy(0, 2, before).wait_send()
+
+    @pl.when(has_after)
+    def _():
+        near_copy(4, 3, after).wait_send()
+
+
+def back_scatter(x_win, seg_query, seg_keys, gathered, queries, key_win, value_win, att_grad, logs, delta, mid_grad, parts, plan):
+    where, block = plan[:2]
+    window, rows = x_win.shape[0], queries.shape[0]
+    seg_keys = jnp.broadcast_to(seg_keys, (window, LANES))
+    count = lax.axis_size("fsdp")
+    depth = count // 8
+    hot, cold = transfer_pieces(plan, depth)
+    early = sorted(cold, reverse=True)
+    late = []
+    for piece in sorted(hot, reverse=True):
+        late += cut(piece, 4) if piece[2] > block // 2 else [piece]
+    many = len(early) + len(late)
+    dma = pltpu.SemaphoreType.DMA
+    tiles = lambda *n: pltpu.VMEM((*n, ROWS, LANES), BF)
+    vm = lambda a, b, t: pltpu.VMEM((a, b), t)
+    hbm = lambda *n: jax.ShapeDtypeStruct((*n, ROWS, LANES), BF)
+    return pl.pallas_call(
+        functools.partial(back_scatter_kernel, depth, where, early, late),
+        out_shape=(
+            jax.ShapeDtypeStruct(parts.shape, BF), jax.ShapeDtypeStruct((block, ROWS, LANES), F32), jax.ShapeDtypeStruct((rows, D), BF),
+            hbm(depth, 4, block), hbm(depth, 4, block), hbm(depth, 2, block), hbm(depth, 2, block), hbm(depth + 1, block),
+            jax.ShapeDtypeStruct((5, rows, D), BF), jax.ShapeDtypeStruct((4, rows, D), BF),
+        ),
+        in_specs=[ANY, VM, VM, ANY, VM, ANY, ANY, VM, VM, VM, ANY, ANY],
+        out_specs=[ANY, VM, VM] + [ANY] * 7,
+        scratch_shapes=[
+            tiles(3, D // ROWS, DC), tiles(2, D // ROWS, DC), tiles(2), tiles(2),
+            vm(window, rows, BF), vm(window, rows, BF), vm(D, window, BF), vm(window, D, BF), vm(window, D, BF),
+            vm(D, rows, F32), vm(PAIR, rows, F32), vm(LANES, rows, F32), vm(window, D, BF), vm(rows, D, F32), vm(rows // 3, D, F32),
+            vm(1, D, F32), vm(D, LANES, F32), vm(D, LANES, F32), tiles(6, block), tiles(block),
+            dma((many, 4)), dma((many, 4)), dma((many, 2)), dma((many, 2)), dma((many, 2)), dma((many, 2)), dma((many,)), dma((many, 2)),
+            dma((4,)), dma((4,)), dma((2,)), dma((2,)), dma((4,)), dma, dma((4,)), dma,
+        ],
+        input_output_aliases={11: 0},
+        compiler_params=pltpu.CompilerParams(collective_id=1, has_side_effects=True, vmem_limit_bytes=VMEM_LIMIT),
+        name="back_scatter",
+    )(x_win, seg_query, seg_keys, gathered, queries, key_win, value_win, att_grad, logs, delta, mid_grad, parts)[1:3]
 
 
 def passed_along(value, steps):
@@ -1446,27 +1747,31 @@
     where = plan[0]
     block = to_tiles(params, plan)
     if kernels:
-        gathered, x_win, _, queries, key_win, value_win, attended, logs = gather_front(
+        gathered, x_win, _, queries, key_win, value_win, attended, rest, logs = gather_front(
             block, block_input, seg_query[:, None], seg_keys[None, :], plan
         )
     else:
         x_win = window_of(block_input)
         gathered = lax.all_gather(block, "fsdp", axis=0, tiled=False)
-        queries, key_win, value_win, attended, logs = front(
+        queries, key_win, value_win, attended, rest, logs = front(
             x_win, seg_query[:, None], seg_keys[None, :], gathered, where, rows
         )
-    activations, mid_grad, att_grad, parts = middle(block_input, cotangent, attended, gathered, where)
-    near, own, parts = back(
-        x_win, seg_query[None, :], seg_keys[:, None], gathered, queries, key_win, value_win, att_grad, logs, parts, where
-    )
-    input_grad = mid_grad + own
-    for k in range(-REACH, REACH + 1):
-        if k != 0:
-            part = near[(k + REACH) * rows : (k + REACH + 1) * rows]
-            input_grad = input_grad + passed_along(part, k).astype(jnp.float32)
-    summed = scatter_blocks(parts, kernels)
+    activations, mid_grad, att_grad, delta, parts = middle(block_input, cotangent, attended, rest, gathered, where)
+    sides = (x_win, seg_query[None, :], seg_keys[:, None], gathered, queries, key_win, value_win, att_grad, logs)
+    if kernels:
+        summed, input_grad = back_scatter(*sides, delta, mid_grad, parts, plan)
+    else:
+        near, own, parts = back(*sides, parts, where)
+        input_grad = mid_grad + own
+        for k in range(-REACH, REACH + 1):
+            if k != 0:
+                part = near[(k + REACH) * rows : (k + REACH + 1) * rows]
+                input_grad = input_grad + passed_along(part, k).astype(jnp.float32)
+        input_grad = input_grad.astype(jnp.bfloat16)
+        received = lax.all_to_all(parts, "fsdp", split_axis=0, concat_axis=0, tiled=True)
+        summed = jnp.sum(received.astype(jnp.float32), axis=0)
     param_grads = to_flat(summed, plan, params.shape[1])
-    return (activations, input_grad.astype(jnp.bfloat16), param_grads)
+    return (activations, input_grad, param_grads)
 
 
 def two_by_two(mesh):

time: 621 us -> 533 us (0.86)
  the two profiles are of different devices: /device:TPU:3 before, /device:TPU:4 now
where the time goes in v2:
time: 533 us; the launch traced here: 524 us
  Pallas kernels  502 us (94%)
  local copies, waits for them, and re-layouts  10.7 us (2%)
  waiting for transfers between devices  6.5 us (1%)
    pallas_call x1, Pallas kernels, back_scatter(): pl.pallas_call(functools.partial(back_scatter_kernel, depth, where, early...  231 us
    pallas_call x1, Pallas kernels, gather_front(): pl.pallas_call(functools.partial(gather_front_kernel, depth, where, early...  197 us
    pallas_call x1, Pallas kernels, middle(): pl.pallas_call(functools.partial(middle_kernel, where), out_shape=(shape(...  57.8 us
  transfers between devices with their start and end apart: 2, of which 1 were waited for; matrix products, arithmetic and copies ran while one was open for 1% of the time, Pallas kernels for 0%

profile of v2, /device:TPU:4, one launch (start us, length us, event | category | flops | bytes accessed | tf_op | source)
XLA Modules:
  0.0 524.0 jit_solution(14817624089631842082)
XLA Ops:
  0.6 1.2 slice.6
  1.9 0.9 collective-permute-start
  2.8 0.8 pad_dynamic-slice_fusion
  3.6 0.8 dynamic_slice.16
  4.4 0.5 broadcast_in_dim.17.segq_ref
  4.9 0.8 broadcast_in_dim.19.segq_ref
  5.7 0.6 broadcast_in_dim.16.segk_ref
  6.3 1.3 dynamic-slice_bitcast_fusion.table_ref
  7.6 0.0 collective-permute-done.head_ref
  7.6 0.0 copy-start
  7.6 0.7 copy-done
  8.3 7.8 %to_tiles.1.block_ref = bf16[242,16,128]{2,1,0:T(8,128)(2,1)} custom-call(s32[81]{0:T(128)} %dynamic-slice_bitcast_fusion.table_ref, bf16[1,476288]{1,0:T(2,128)(2,1)} %line_ref.1, bf16[1,69632]{1,0:T(2,128)(2,1)} %copy-done), custom_call_target="tpu_custom_call" | custom-call | tf_op jit(solution)/shard_map/to_tiles/pallas_call | solution.py:239
  16.1 197.4 %gather_front.1 = (bf16[32,242,16,128]{3,2,1,0:T(8,128)(2,1)}, bf16[1920,1152]{1,0:T(8,128)(2,1)}, bf16[5,384,1152]{2,1,0:T(8,128)(2,1)}, bf16[384,1152]{1,0:T(8...) custom-call(bf16[242,16,128]{2,1,0:T(8,128)(2,1)} %to_tiles.1.block_, ...), custom_call_target="tpu_custom_call" | custom-call | tf_op jit(solution)/shard_map/gather_front/pallas_call | solution.py:1196
  213.5 57.8 %middle.1 = (bf16[384,1152]{1,0:T(8,128)(2,1)}, f32[384,1152]{1,0:T(8,128)}, bf16[384,1152]{1,0:T(8,128)(2,1)}, f32[16,384]{1,0:T(8,128)}, bf16[32,242,16,128]{3,2,1,0:T(8,128)(2,1)}) custom-call(bf16[384,1152]{1,0:T(8,128)(2,1)} %x_ref.1, bf16[384,1152]{1,0:T(8,128)(2,1)} %cot_ref.1, bf16[384,1152]{1,0:T(8,128)(2,1)} %get-tuple-element.20.attended_ref, ...), custom_call_target="tpu_custom_call" | custom-call | tf_op jit(solution)/shard_map/middle/pallas_call | solution.py:611
  271.3 1.3 broadcast_in_dim.18.segk_ref
  272.6 0.0 copy-start.1
  272.6 231.0 %back_scatter.1 = (bf16[32,242,16,128]{3,2,1,0:T(8,128)(2,1)}, f32[242,16,128]{2,1,0:T(8,128)}, bf16[384,1152]{1,0:T(8,128)(2,1)}, bf16[4,4,242,16,128]{4,3,2,1,...) custom-call(bf16[1920,1152]{1,0:T(8,128)(2,1)} %get-tuple-element.24, ...), custom_call_target="tpu_custom_call", output_to_operand_aliasing={{0}: (11, {})} | custom-call | tf_op jit(solution)/shard_map/back_scatter/pallas_call | solution.py:1704
  503.6 8.4 %to_flat.1 = (f32[1,476288]{1,0:T(1,128)}, f32[1,69632]{1,0:T(1,128)}) custom-call(s32[81]{0:T(128)} %dynamic-slice_bitcast_fusion.table_ref, f32[242,16,128]{2,1,0:T(8,128)} %get-tuple-element.34.tile_ref), custom_call_target="tpu_custom_call" | custom-call | tf_op jit(solution)/shard_map/to_flat/pallas_call | solution.py:254
  511.9 0.0 collective-permute-start.1
  511.9 0.0 copy-done.1
  511.9 0.6 dynamic_slice.18
  512.5 6.5 %collective-permute-done.1 = f32[1,69632]{1,0:T(1,128)S(1)} collective-permute-done((f32[1,69632]{1,0:T(1,128)}, f32[1,69632]{1,0:T(1,128)S(1)}, u32[]{:S(2)}, u32[]{:S(2)}) %collective-permute-start.1) | collective-permute-done | bytes 278560 | tf_op jit(solution)/shard_map/ppermute | solution.py:263
  519.0 2.6 fusion
  521.6 2.1 copy.14
Async XLA Ops:
  1.9 5.7 %collective-permute-start = (bf16[1,69632]{1,0:T(2,128)(2,1)S(1)}, bf16[1,69632]{1,0:T(2,128)(2,1)S(1)}, u32[]{:S(2)}, u32[]{:S(2)}) collective-permute-start(bf16[1,69632]{1,0:T(2,128)(2,1)S(1)} %slice.6), channel_id=1, source_target_pairs={{0,31},{1,0},{2,1},{3,2},{4,3},{5,4},{6,5},{7,6},{8,7},{9,8},{10,9... | collective-permute-start | bytes 417800 | tf_op jit(solution)/shard_map/ppermute | solution.py:237
  7.6 0.7 copy-start
  272.6 239.4 %copy-start.1 = (s32[32]{0:T(128)S(1)}, s32[32]{0:T(128)}, u32[]{:S(2)}) copy-start(s32[32]{0:T(128)} %constant.30.clone) | copy-start | bytes 388
  511.9 7.1 %collective-permute-start.1 = (f32[1,69632]{1,0:T(1,128)}, f32[1,69632]{1,0:T(1,128)S(1)}, u32[]{:S(2)}, u32[]{:S(2)}) collective-permute-start(f32[1,69632]{1,0:T(1,128)} %get-tuple-element.36), channel_id=1, source_target_pairs={{0,1},{1,2},{2,3},{3,4},{4,5},{5,6},{6,7},{7,8},{8,9},{9,10},{10,1... | collective-permute-start | bytes 835592 | tf_op jit(solution)/shard_map/ppermute | solution.py:263
